TPU v7x, 32 devices: a whole 2x2x4 slice. The times are simulated.
32 devices in a mesh: dp: 2 (over x), sx: 4 (over z), sy: 4 (over y, core).
Axes of the slice: x: 2, y: 2, z: 4, core: 2. Of those that a mesh axis runs over, the one named last changes fastest.
Arguments:
- act_in: bfloat16 [32, 384, 64, 256], P('dp', 'sy', 'sx'), parts along dimension 0
- norm_first: bfloat16 [2, 256], replicated
- w_first: bfloat16 [3, 3, 256, 128], replicated
- w_short: bfloat16 [256, 128], replicated
- norm_rest: bfloat16 [6, 2, 128], replicated
- w_rest: bfloat16 [5, 3, 3, 128, 128], replicated
- bias_rest: bfloat16 [7, 128], replicated
- w_out: bfloat16 [3, 3, 128, 3], replicated
- bias_out: bfloat16 [3], replicated
Outputs:
- output: float32 [32, 384, 64, 3], P('dp', 'sy', 'sx'), parts along dimension 0
There are 2 independent parts. A program takes and returns all parts, laid end to end along the dimension named above; an argument that names none is the same for every part.
All inputs are finite; a program needn't handle non-finite values.
Results may differ from a plain program's by a relative error of at most 0.00891096.
Values are sent between devices in bfloat16 or wider.
A program may use at most 1 GiB of HBM per device.

v0:
```python
import jax
import jax.numpy as jnp
from jax import lax
from jax.sharding import PartitionSpec as P

GROUPS = 32
GN_EPS = 1e-6


def solution(mesh):
    rows_n = mesh.shape["sy"]
    cols_n = mesh.shape["sx"]
    to_below = [(position, position + 1) for position in range(rows_n - 1)]
    to_above = [(position + 1, position) for position in range(rows_n - 1)]
    to_right = [(position, position + 1) for position in range(cols_n - 1)]
    to_left = [(position + 1, position) for position in range(cols_n - 1)]
    tile_spec = P("dp", "sy", "sx", None)
    replicated = P()

    def add_border(act_map):
        top_row = lax.ppermute(act_map[:, -1:], "sy", to_below)
        bottom_row = lax.ppermute(act_map[:, :1], "sy", to_above)
        tall = jnp.concatenate([top_row, act_map, bottom_row], axis=1)
        left_col = lax.ppermute(tall[:, :, -1:], "sx", to_right)
        right_col = lax.ppermute(tall[:, :, :1], "sx", to_left)
        return jnp.concatenate([left_col, tall, right_col], axis=2)

    def conv_tile(act_map, kernel):
        return lax.conv_general_dilated(add_border(act_map), kernel, (1, 1), ((0, 0), (0, 0)), dimension_numbers=("NHWC", "HWIO", "NHWC"), preferred_element_type=jnp.float32)

    def group_norm_act(act_map, norm_pair):
        samples = act_map.shape[0]
        per_group = act_map.shape[3] // GROUPS
        group_count = act_map.shape[1] * rows_n * act_map.shape[2] * cols_n * per_group
        sum_one = jnp.sum(act_map, axis=(1, 2), dtype=jnp.float32).reshape(samples, GROUPS, per_group).sum(axis=2)
        sum_two = jnp.sum(jnp.square(act_map.astype(jnp.float32)), axis=(1, 2)).reshape(samples, GROUPS, per_group).sum(axis=2)
        totals = lax.psum(jnp.stack([sum_one, sum_two], axis=-1), ("sy", "sx"))
        group_mean = totals[:, :, 0] / group_count
        inv_std = lax.rsqrt(totals[:, :, 1] / group_count - group_mean * group_mean + GN_EPS)
        chan_scale = jnp.repeat(inv_std, per_group, axis=1) * norm_pair[0].astype(jnp.float32)
        chan_shift = norm_pair[1].astype(jnp.float32) - jnp.repeat(group_mean, per_group, axis=1) * chan_scale
        return jax.nn.silu(act_map.astype(jnp.float32) * chan_scale[:, None, None, :] + chan_shift[:, None, None, :]).astype(jnp.bfloat16)

    def local_decode(act_in, norm_first, w_first, w_short, norm_rest, w_rest, bias_rest, w_out, bias_out):
        bias_rows = bias_rest.astype(jnp.float32)
        mid_act = (conv_tile(group_norm_act(act_in, norm_first), w_first) + bias_rows[0]).astype(jnp.bfloat16)
        skip_path = jnp.einsum("nhwc,cd->nhwd", act_in, w_short, preferred_element_type=jnp.float32) + bias_rows[6]
        hidden = (conv_tile(group_norm_act(mid_act, norm_rest[0]), w_rest[0]) + bias_rows[1] + skip_path).astype(jnp.bfloat16)
        for res_index in range(1, 3):
            first_at = 2 * res_index - 1
            mid_act = (conv_tile(group_norm_act(hidden, norm_rest[first_at]), w_rest[first_at]) + bias_rows[first_at + 1]).astype(jnp.bfloat16)
            hidden = (conv_tile(group_norm_act(mid_act, norm_rest[first_at + 1]), w_rest[first_at + 1]) + bias_rows[first_at + 2] + hidden.astype(jnp.float32)).astype(jnp.bfloat16)
        return conv_tile(group_norm_act(hidden, norm_rest[5]), w_out) + bias_out.astype(jnp.float32)

    return jax.shard_map(local_decode, mesh=mesh, in_specs=(tile_spec, replicated, replicated, replicated, replicated, replicated, replicated, replicated, replicated), out_specs=tile_spec, check_vma=False)
```

profile of v0, /device:TPU:0, one launch (start us, length us, event | category | flops | bytes accessed | tf_op | source)
XLA Modules:
  0.0 850.2 jit_solution(5335371430890332685)
XLA Ops:
  0.0 17.8 %convert_reduce_fusion = (f32[16,256]{1,0:T(8,128)S(1)}, f32[16,256]{1,0:T(8,128)S(1)}) fusion(bf16[16,96,16,256]{3,2,1,0:T(8,128)(2,1)} %param.9), kind=kLoop, calls=%fused_computation.2 | loop fusion | flops 25157632 | bytes 12615680 | tf_op jit(solution)/shard_map/reduce_sum | solution.py:35
  18.1 63.4 %psum.49 = f32[16,32,2]{0,1,2:T(8,128)S(1)} all-reduce(f32[16,32,2]{0,1,2:T(8,128)S(1)} %pad_maximum_fusion.21), channel_id=1, replica_groups=mesh['dp'=2,'sx'=4,'sy'=4] {'sy','sx'}, use_global_device_ids=true, to_apply=%region_4.0 | all-reduce | flops 1024 | bytes 8192 | tf_op jit(solution)/shard_map/psum | solution.py:37
  81.8 25.3 %fusion.7 = bf16[16,96,16,256]{3,0,2,1:T(8,128)(2,1)S(1)} fusion(f32[16,256]{1,0:T(8,128)S(1)} %get-tuple-element.31, f32[16,256]{1,0:T(8,128)S(1)} %get-tuple-element.32, bf16[16,96,16,256]{3,2,1,0:T(8,128)(2,1)} %param.9), kind=kLoop, calls=%fused_computation.10 | loop fusion | flops 50331648 | bytes 25198592 | tf_op jit(solution)/shard_map/convert_element_type | solution.py:42
  116.8 12.4 %collective-permute-done.2 = bf16[16,98,1,256]{3,0,2,1:T(8,128)(2,1)S(1)} collective-permute-done((bf16[16,98,1,256]{3,0,2,1:T(8,128)(2,1)S(1)}, bf16[16,98,1,256]{3,0,2,1:T(8,128)(2,1)S(1)}, u32[]{:S(2)}, u32[]{:S(2)}) %collective-permute-start.2) | collective-permute-done | bytes 802848 | tf_op jit(solution)/shard_map/ppermute | solution.py:24
  134.0 32.0 %convert_reduce_fusion.6 = (f32[16,128]{1,0:T(8,128)S(1)}, f32[16,128]{1,0:T(8,128)S(1)}, bf16[16,96,16,128]{3,0,2,1:T(8,128)(2,1)}) fusion(f32[128]{0:T(128)S(1)} %get-tuple-element.67, bf16[3,3,256,128]{3,2,1,0:T(8,128)(2,1)S(1)} %copy-done, bf16[16,98,1,256]{3,0,2,1:T(8,128)(2,1)S(1)} %collective-permute-done.3, ...), kind=kOutput, calls=%fused_computation.30 | convolution fusion | flops 14543286272 | bytes 21348864 | tf_op jit(solution)/shard_map/conv_general_dilated | solution.py:29
  166.2 58.8 %psum.50 = f32[16,32,2]{0,1,2:T(8,128)S(1)} all-reduce(f32[16,32,2]{0,1,2:T(8,128)S(1)} %pad_maximum_fusion.22), channel_id=1, replica_groups=mesh['dp'=2,'sx'=4,'sy'=4] {'sy','sx'}, use_global_device_ids=true, to_apply=%region_9.10 | all-reduce | flops 1024 | bytes 8192 | tf_op jit(solution)/shard_map/psum | solution.py:37
  240.9 12.8 %fusion.68 = f32[16,96,16,128]{3,0,2,1:T(8,128)S(1)} fusion(bf16[16,96,16,256]{3,2,1,0:T(8,128)(2,1)} %param.9, bf16[256,128]{1,0:T(8,128)(2,1)S(1)} %copy-done.3), kind=kOutput, calls=%fused_computation.95 | convolution fusion | flops 1610612736 | bytes 25231360 | tf_op jit(solution)/shard_map/nhwc,cd->nhwd/dot_general | solution.py:47
  253.7 19.3 %convert_reduce_fusion.2 = (f32[16,128]{1,0:T(8,128)S(1)}, f32[16,128]{1,0:T(8,128)S(1)}, bf16[16,96,16,128]{3,0,2,1:T(8,128)(2,1)}) fusion(f32[16,96,16,128]{3,0,2,1:T(8,128)S(1)} %fusion.68, f32[128]{0:T(128)S(1)} %get-tuple-element.65, f32[128]{0:T(128)S(1)} %get-tuple-element.66, bf16[5,3,3,128,128]{4,3,2,1,0:T(8,128)(2,1)} %param.14, ...), kind=kOutput, calls=%fused_computation.18 | convolution fusion | flops 7287369728 | bytes 26412032 | tf_op jit(solution)/shard_map/conv_general_dilated | solution.py:29
  273.3 60.4 %psum.51 = f32[16,32,2]{0,1,2:T(8,128)S(1)} all-reduce(f32[16,32,2]{0,1,2:T(8,128)S(1)} %pad_maximum_fusion.23), channel_id=1, replica_groups=mesh['dp'=2,'sx'=4,'sy'=4] {'sy','sx'}, use_global_device_ids=true, to_apply=%region_14.15 | all-reduce | flops 1024 | bytes 8192 | tf_op jit(solution)/shard_map/psum | solution.py:37
  350.3 5.9 collective-permute-done.10
  360.9 17.6 %convert_reduce_fusion.5 = (f32[16,128]{1,0:T(8,128)S(1)}, f32[16,128]{1,0:T(8,128)S(1)}, bf16[16,96,16,128]{3,0,2,1:T(8,128)(2,1)}) fusion(f32[128]{0:T(128)S(1)} %get-tuple-element.64, bf16[5,3,3,128,128]{4,3,2,1,0:T(8,128)(2,1)} %param.14, bf16[16,98,1,128]{3,0,2,1:T(8,128)(2,1)S(1)} %collective-permute-done.11, ...), kind=kOutput, calls=%fused_computation.27 | convolution fusion | flops 7281078272 | bytes 13828608 | tf_op jit(solution)/shard_map/conv_general_dilated | solution.py:29
  378.8 59.0 %psum.52 = f32[16,32,2]{0,1,2:T(8,128)S(1)} all-reduce(f32[16,32,2]{0,1,2:T(8,128)S(1)} %pad_maximum_fusion.24), channel_id=1, replica_groups=mesh['dp'=2,'sx'=4,'sy'=4] {'sy','sx'}, use_global_device_ids=true, to_apply=%region_19.20 | all-reduce | flops 1024 | bytes 8192 | tf_op jit(solution)/shard_map/psum | solution.py:37
  438.0 5.8 fusion.33
  453.1 6.1 collective-permute-done.14
  464.0 18.1 %convert_reduce_fusion.1 = (f32[16,128]{1,0:T(8,128)S(1)}, f32[16,128]{1,0:T(8,128)S(1)}, bf16[16,96,16,128]{3,0,2,1:T(8,128)(2,1)}) fusion(bf16[16,96,16,128]{3,0,2,1:T(8,128)(2,1)S(1)} %bitcast.215, f32[128]{0:T(128)S(1)} %get-tuple-element.63, bf16[5,3,3,128,128]{4,3,2,1,0:T(8,128)(2,1)} %param.14, ...), kind=kOutput, calls=%fused_computation.14 | convolution fusion | flops 7287369728 | bytes 20120064 | tf_op jit(solution)/shard_map/conv_general_dilated | solution.py:29
  482.4 58.3 %psum.53 = f32[16,32,2]{0,1,2:T(8,128)S(1)} all-reduce(f32[16,32,2]{0,1,2:T(8,128)S(1)} %pad_maximum_fusion.25), channel_id=1, replica_groups=mesh['dp'=2,'sx'=4,'sy'=4] {'sy','sx'}, use_global_device_ids=true, to_apply=%region_24.25 | all-reduce | flops 1024 | bytes 8192 | tf_op jit(solution)/shard_map/psum | solution.py:37
  556.1 5.9 collective-permute-done.18
  566.7 17.6 %convert_reduce_fusion.4 = (f32[16,128]{1,0:T(8,128)S(1)}, f32[16,128]{1,0:T(8,128)S(1)}, bf16[16,96,16,128]{3,0,2,1:T(8,128)(2,1)}) fusion(f32[128]{0:T(128)S(1)} %copy-done.14, bf16[5,3,3,128,128]{4,3,2,1,0:T(8,128)(2,1)} %param.14, bf16[16,98,1,128]{3,0,2,1:T(8,128)(2,1)S(1)} %collective-permute-done.19, ...), kind=kOutput, calls=%fused_computation.24 | convolution fusion | flops 7281078272 | bytes 13828608 | tf_op jit(solution)/shard_map/conv_general_dilated | solution.py:29
  584.6 58.4 %psum.54 = f32[16,32,2]{0,1,2:T(8,128)S(1)} all-reduce(f32[16,32,2]{0,1,2:T(8,128)S(1)} %pad_maximum_fusion.26), channel_id=1, replica_groups=mesh['dp'=2,'sx'=4,'sy'=4] {'sy','sx'}, use_global_device_ids=true, to_apply=%region_29.30 | all-reduce | flops 1024 | bytes 8192 | tf_op jit(solution)/shard_map/psum | solution.py:37
  658.3 6.2 collective-permute-done.22
  669.2 18.1 %convert_reduce_fusion.3 = (f32[16,128]{1,0:T(8,128)S(1)}, f32[16,128]{1,0:T(8,128)S(1)}, bf16[16,96,16,128]{3,0,2,1:T(8,128)(2,1)}) fusion(bf16[16,96,16,128]{3,0,2,1:T(8,128)(2,1)S(1)} %bitcast.217, f32[128]{0:T(128)S(1)} %copy-done.13, bf16[5,3,3,128,128]{4,3,2,1,0:T(8,128)(2,1)} %param.14, bf16[16,98,1,128]{3,0,2,1:T(8,128)(2,1)S(1)} %collective-permute-done.23, ...), kind=kOutput, calls=%fused_computation.21 | convolution fusion | flops 7287369728 | bytes 20120064 | tf_op jit(solution)/shard_map/conv_general_dilated | solution.py:29
  687.6 58.2 %psum.55 = f32[16,32,2]{0,1,2:T(8,128)S(1)} all-reduce(f32[16,32,2]{0,1,2:T(8,128)S(1)} %pad_maximum_fusion.27), channel_id=1, replica_groups=mesh['dp'=2,'sx'=4,'sy'=4] {'sy','sx'}, use_global_device_ids=true, to_apply=%region_34.35 | all-reduce | flops 1024 | bytes 8192 | tf_op jit(solution)/shard_map/psum | solution.py:37
  760.8 6.3 collective-permute-done.26
  771.9 74.6 %fusion.142 = f32[16,96,16,3]{0,3,2,1:T(4,128)} fusion(bf16[3,3,128,3]{2,3,1,0:T(4,128)(2,1)S(1)} %copy-done.15, bf16[16,98,1,128]{3,0,2,1:T(8,128)(2,1)S(1)} %collective-permute-done.27, bf16[16,1,16,128]{3,0,2,1:T(8,128)(2,1)S(1)} %collective-permute-done.25, bf16[16,96,16,128]{3,0,2,1:T(8,128)(2,1)S(1)} %fusion.49, ...), kind=kOutput, calls=%fused_computation.157 | convolution fusion | flops 184393728 | bytes 7527180 | tf_op jit(solution)/shard_map/conv_general_dilated | solution.py:29
  (203 shorter events, 130.8 us)
Async XLA Ops:
  107.1 2.6 collective-permute-start
  108.4 3.9 collective-permute-start.1
  112.5 16.7 %collective-permute-start.2 = (bf16[16,98,1,256]{3,0,2,1:T(8,128)(2,1)S(1)}, bf16[16,98,1,256]{3,0,2,1:T(8,128)(2,1)S(1)}, u32[]{:S(2)}, u32[]{:S(2)}) collective-permute-start(bf16[16,98,1,256]{3,0,2,1:T(8,128)(2,1)S(1)} %get-tuple-element.33), channel_id=1, source_target_pairs={{0,4},{4,8},{8,12},{1,5},{5,9},{9,13},{2,6},{6,10},{10,14},{3,7},{... | collective-permute-start | bytes 2408456 | tf_op jit(solution)/shard_map/ppermute | solution.py:24
  113.9 20.1 %collective-permute-start.3 = (bf16[16,98,1,256]{3,0,2,1:T(8,128)(2,1)S(1)}, bf16[16,98,1,256]{3,0,2,1:T(8,128)(2,1)S(1)}, u32[]{:S(2)}, u32[]{:S(2)}) collective-permute-start(bf16[16,98,1,256]{3,0,2,1:T(8,128)(2,1)S(1)} %get-tuple-element.34), channel_id=1, source_target_pairs={{4,0},{8,4},{12,8},{5,1},{9,5},{13,9},{6,2},{10,6},{14,10},{7,3},{... | collective-permute-start | bytes 2408456 | tf_op jit(solution)/shard_map/ppermute | solution.py:25
  231.0 2.6 collective-permute-start.4
  232.3 5.3 collective-permute-start.5
  237.7 16.0 %collective-permute-start.6 = (bf16[16,98,1,128]{3,0,2,1:T(8,128)(2,1)S(1)}, bf16[16,98,1,128]{3,0,2,1:T(8,128)(2,1)S(1)}, u32[]{:S(2)}, u32[]{:S(2)}) collective-permute-start(bf16[16,98,1,128]{3,0,2,1:T(8,128)(2,1)S(1)} %get-tuple-element.47), channel_id=1, source_target_pairs={{0,4},{4,8},{8,12},{1,5},{5,9},{9,13},{2,6},{6,10},{10,14},{3,7},{... | collective-permute-start | bytes 1204232 | tf_op jit(solution)/shard_map/ppermute | solution.py:24
  239.4 14.3 %collective-permute-start.7 = (bf16[16,98,1,128]{3,0,2,1:T(8,128)(2,1)S(1)}, bf16[16,98,1,128]{3,0,2,1:T(8,128)(2,1)S(1)}, u32[]{:S(2)}, u32[]{:S(2)}) collective-permute-start(bf16[16,98,1,128]{3,0,2,1:T(8,128)(2,1)S(1)} %get-tuple-element.48), channel_id=1, source_target_pairs={{4,0},{8,4},{12,8},{5,1},{9,5},{13,9},{6,2},{10,6},{14,10},{7,3},{... | collective-permute-start | bytes 1204232 | tf_op jit(solution)/shard_map/ppermute | solution.py:25
  341.0 6.4 collective-permute-start.9
  347.5 8.7 %collective-permute-start.10 = (bf16[16,98,1,128]{3,0,2,1:T(8,128)(2,1)S(1)}, bf16[16,98,1,128]{3,0,2,1:T(8,128)(2,1)S(1)}, u32[]{:S(2)}, u32[]{:S(2)}) collective-permute-start(bf16[16,98,1,128]{3,0,2,1:T(8,128)(2,1)S(1)} %get-tuple-element.45), channel_id=1, source_target_pairs={{0,4},{4,8},{8,12},{1,5},{5,9},{9,13},{2,6},{6,10},{10,14},{3,7},{... | collective-permute-start | bytes 1204232 | tf_op jit(solution)/shard_map/ppermute | solution.py:24
  348.8 12.1 %collective-permute-start.11 = (bf16[16,98,1,128]{3,0,2,1:T(8,128)(2,1)S(1)}, bf16[16,98,1,128]{3,0,2,1:T(8,128)(2,1)S(1)}, u32[]{:S(2)}, u32[]{:S(2)}) collective-permute-start(bf16[16,98,1,128]{3,0,2,1:T(8,128)(2,1)S(1)} %get-tuple-element.46), channel_id=1, source_target_pairs={{4,0},{8,4},{12,8},{5,1},{9,5},{13,9},{6,2},{10,6},{14,10},{7,3},{... | collective-permute-start | bytes 1204232 | tf_op jit(solution)/shard_map/ppermute | solution.py:25
  445.1 4.7 collective-permute-start.13
  450.0 9.3 %collective-permute-start.14 = (bf16[16,98,1,128]{3,0,2,1:T(8,128)(2,1)S(1)}, bf16[16,98,1,128]{3,0,2,1:T(8,128)(2,1)S(1)}, u32[]{:S(2)}, u32[]{:S(2)}) collective-permute-start(bf16[16,98,1,128]{3,0,2,1:T(8,128)(2,1)S(1)} %get-tuple-element.43), channel_id=1, source_target_pairs={{0,4},{4,8},{8,12},{1,5},{5,9},{9,13},{2,6},{6,10},{10,14},{3,7},{... | collective-permute-start | bytes 1204232 | tf_op jit(solution)/shard_map/ppermute | solution.py:24
  451.6 12.4 %collective-permute-start.15 = (bf16[16,98,1,128]{3,0,2,1:T(8,128)(2,1)S(1)}, bf16[16,98,1,128]{3,0,2,1:T(8,128)(2,1)S(1)}, u32[]{:S(2)}, u32[]{:S(2)}) collective-permute-start(bf16[16,98,1,128]{3,0,2,1:T(8,128)(2,1)S(1)} %get-tuple-element.44), channel_id=1, source_target_pairs={{4,0},{8,4},{12,8},{5,1},{9,5},{13,9},{6,2},{10,6},{14,10},{7,3},{... | collective-permute-start | bytes 1204232 | tf_op jit(solution)/shard_map/ppermute | solution.py:25
  546.5 2.6 collective-permute-start.16
  547.8 4.7 collective-permute-start.17
  552.6 9.3 %collective-permute-start.18 = (bf16[16,98,1,128]{3,0,2,1:T(8,128)(2,1)S(1)}, bf16[16,98,1,128]{3,0,2,1:T(8,128)(2,1)S(1)}, u32[]{:S(2)}, u32[]{:S(2)}) collective-permute-start(bf16[16,98,1,128]{3,0,2,1:T(8,128)(2,1)S(1)} %get-tuple-element.41), channel_id=1, source_target_pairs={{0,4},{4,8},{8,12},{1,5},{5,9},{9,13},{2,6},{6,10},{10,14},{3,7},{... | collective-permute-start | bytes 1204232 | tf_op jit(solution)/shard_map/ppermute | solution.py:24
  554.3 12.4 %collective-permute-start.19 = (bf16[16,98,1,128]{3,0,2,1:T(8,128)(2,1)S(1)}, bf16[16,98,1,128]{3,0,2,1:T(8,128)(2,1)S(1)}, u32[]{:S(2)}, u32[]{:S(2)}) collective-permute-start(bf16[16,98,1,128]{3,0,2,1:T(8,128)(2,1)S(1)} %get-tuple-element.42), channel_id=1, source_target_pairs={{4,0},{8,4},{12,8},{5,1},{9,5},{13,9},{6,2},{10,6},{14,10},{7,3},{... | collective-permute-start | bytes 1204232 | tf_op jit(solution)/shard_map/ppermute | solution.py:25
  650.3 4.7 collective-permute-start.21
  655.1 9.3 %collective-permute-start.22 = (bf16[16,98,1,128]{3,0,2,1:T(8,128)(2,1)S(1)}, bf16[16,98,1,128]{3,0,2,1:T(8,128)(2,1)S(1)}, u32[]{:S(2)}, u32[]{:S(2)}) collective-permute-start(bf16[16,98,1,128]{3,0,2,1:T(8,128)(2,1)S(1)} %get-tuple-element.39), channel_id=1, source_target_pairs={{0,4},{4,8},{8,12},{1,5},{5,9},{9,13},{2,6},{6,10},{10,14},{3,7},{... | collective-permute-start | bytes 1204232 | tf_op jit(solution)/shard_map/ppermute | solution.py:24
  656.8 12.4 %collective-permute-start.23 = (bf16[16,98,1,128]{3,0,2,1:T(8,128)(2,1)S(1)}, bf16[16,98,1,128]{3,0,2,1:T(8,128)(2,1)S(1)}, u32[]{:S(2)}, u32[]{:S(2)}) collective-permute-start(bf16[16,98,1,128]{3,0,2,1:T(8,128)(2,1)S(1)} %get-tuple-element.40), channel_id=1, source_target_pairs={{4,0},{8,4},{12,8},{5,1},{9,5},{13,9},{6,2},{10,6},{14,10},{7,3},{... | collective-permute-start | bytes 1204232 | tf_op jit(solution)/shard_map/ppermute | solution.py:25
  753.0 4.7 collective-permute-start.25
  757.8 9.3 %collective-permute-start.26 = (bf16[16,98,1,128]{3,0,2,1:T(8,128)(2,1)S(1)}, bf16[16,98,1,128]{3,0,2,1:T(8,128)(2,1)S(1)}, u32[]{:S(2)}, u32[]{:S(2)}) collective-permute-start(bf16[16,98,1,128]{3,0,2,1:T(8,128)(2,1)S(1)} %get-tuple-element.37), channel_id=1, source_target_pairs={{0,4},{4,8},{8,12},{1,5},{5,9},{9,13},{2,6},{6,10},{10,14},{3,7},{... | collective-permute-start | bytes 1204232 | tf_op jit(solution)/shard_map/ppermute | solution.py:24
  759.5 12.4 %collective-permute-start.27 = (bf16[16,98,1,128]{3,0,2,1:T(8,128)(2,1)S(1)}, bf16[16,98,1,128]{3,0,2,1:T(8,128)(2,1)S(1)}, u32[]{:S(2)}, u32[]{:S(2)}) collective-permute-start(bf16[16,98,1,128]{3,0,2,1:T(8,128)(2,1)S(1)} %get-tuple-element.38), channel_id=1, source_target_pairs={{4,0},{8,4},{12,8},{5,1},{9,5},{13,9},{6,2},{10,6},{14,10},{7,3},{... | collective-permute-start | bytes 1204232 | tf_op jit(solution)/shard_map/ppermute | solution.py:25
  (25 other events, 1414.9 us)
where the time goes:
time: 861 us; the launch traced here: 850 us
  blocking collectives  416 us (48%)
  matrix products  210 us (24%)
  waiting for transfers between devices  96.4 us (11%)
  other arithmetic  79.7 us (9%)
  starting transfers between devices  39.8 us (5%)
    psum x7, blocking collectives, group_norm_act(): totals = lax.psum(jnp.stack([sum_one, sum_two], axis=-1), ('sy', 'sx'))  416 us
    conv_general_dilated x7, matrix products, conv_tile(): lax.conv_general_dilated(add_border(act_map), kernel, (1, 1), ((0, 0), (0...  197 us
    convert_element_type x7, other arithmetic, group_norm_act(): jax.nn.silu(act_map.astype(jnp.float32) * chan_scale[:, None, None, :] +...  59.6 us
    ppermute x7, waiting for transfers between devices, add_border(): left_col = lax.ppermute(tall[:, :, -1:], 'sx', to_right)  42.8 us
    ppermute x7, waiting for transfers between devices, add_border(): right_col = lax.ppermute(tall[:, :, :1], 'sx', to_left)  28.3 us
    ppermute x7, waiting for transfers between devices, add_border(): bottom_row = lax.ppermute(act_map[:, :1], 'sy', to_above)  25.2 us
    reduce_sum x8, other arithmetic, group_norm_act(): jnp.sum(act_map, axis=(1, 2), dtype=jnp.float32)  18.1 us
  transfers between devices with their start and end apart: 28, of which 19 were waited for; matrix products, arithmetic and copies ran while one was open for 2% of the time, Pallas kernels for 0%

commit v1 on v0

v1 whole, which is shorter than its diff:
```python
import functools

import jax
import jax.numpy as jnp
from jax import lax
from jax.experimental import pallas as pl
from jax.experimental.pallas import tpu as pltpu
from jax.sharding import PartitionSpec as P

GROUPS = 32
GN_EPS = 1e-6
MESH = pl.DeviceIdType.MESH
F32 = jnp.float32
LANES = 128
WIDE = 256
SUB = 16
BF16 = jnp.bfloat16
SLAB = 48
BLOCK = 8
STEPS = SLAB // BLOCK
CHUNK = 4
DEPTH = 3
CHUNKS = SLAB // CHUNK


def exact_rows(values):
    high = values.astype(BF16).astype(F32)
    rest = values - high
    mid = rest.astype(BF16).astype(F32)
    low = rest - mid
    return jnp.concatenate([high, mid, low, jnp.zeros_like(low)], axis=0).astype(BF16)


def exact_dot(values, ones):
    out = jnp.dot(exact_rows(values), ones, preferred_element_type=F32)
    return (out[0:8] + out[8:SUB]) + out[SUB:24]


def group_matrix(channels, transposed):
    per_group = channels // GROUPS
    shape = (LANES, 2 * channels) if transposed else (2 * channels, LANES)
    chan = lax.broadcasted_iota(jnp.int32, shape, 1 if transposed else 0)
    lane = lax.broadcasted_iota(jnp.int32, shape, 0 if transposed else 1)
    target = jnp.where(chan < channels, chan // per_group, GROUPS + (chan - channels) // per_group)
    return jnp.where(target == lane, 1.0, 0.0).astype(BF16)


def kernel(rows_n, cols_n, act_in, norm_first, w_first, w_short, norm_rest, w_rest, bias_rest, w_out, image,
           stage, raw_a, raw_t, raw_h, act_a, act_t, wf, ws, wr, wo, perm, sum_a, sum_t, cast_a, cast_t,
           col_a, row_a, cor_a, col_t, row_t, cor_t, slots,
           in_sem, wt_sem, col_send, col_recv, row_send, row_recv, cor_send, cor_recv, stat_send, stat_recv):
    peers = rows_n * cols_n
    my_x = lax.axis_index("sx")
    my_y = lax.axis_index("sy")
    me = my_x * rows_n + my_y
    has_side = (my_x > 0, my_x < cols_n - 1)
    has_end = (my_y > 0, my_y < rows_n - 1)
    count = float(rows_n * cols_n * 2 * SLAB * SUB)

    def at(dx, dy):
        return {"sx": my_x + dx, "sy": my_y + dy}

    def peer(index):
        return {"sx": index // rows_n, "sy": lax.rem(index, rows_n)}

    def col_copy(raw, col, par, g, side, start, size):
        src = raw.at[g, pl.ds(start, size), 0 if side == 0 else 7, side]
        dst = col.at[par, g, 1 - side, pl.ds(start, size)]
        return pltpu.make_async_remote_copy(src, dst, col_send.at[par, g, side], col_recv.at[par, g, 1 - side], device_id=at(2 * side - 1, 0), device_id_type=MESH)

    def row_copy(raw, row, par, g, end):
        src = raw.at[g, 0 if end == 0 else SLAB - 1]
        return pltpu.make_async_remote_copy(src, row.at[par, g, 1 - end], row_send.at[par, g, end], row_recv.at[par, g, 1 - end], device_id=at(0, 2 * end - 1), device_id_type=MESH)

    def cor_copy(raw, cor, par, g, end, side):
        src = raw.at[g, 0 if end == 0 else SLAB - 1, 0 if side == 0 else 7, side]
        return pltpu.make_async_remote_copy(src, cor.at[par, g, 1 - end, 1 - side], cor_send.at[par, g, end, side], cor_recv.at[par, g, 1 - end, 1 - side], device_id=at(2 * side - 1, 2 * end - 1), device_id_type=MESH)

    def stat_copy(par, g, offset):
        return pltpu.make_async_remote_copy(slots.at[par, g, me], slots.at[par, g, me], stat_send.at[par, g], stat_recv.at[par, g], device_id=peer(lax.rem(me + offset, peers)), device_id_type=MESH)

    def send_cols(raw, col, par, g, step):
        for side in range(2):
            @pl.when(has_side[side])
            def _():
                col_copy(raw, col, par, g, side, step * BLOCK, BLOCK).start()

    def send_ends(raw, row, cor, par, g):
        for end in range(2):
            @pl.when(has_end[end])
            def _():
                row_copy(raw, row, par, g, end).start()
            for side in range(2):
                @pl.when(jnp.logical_and(has_end[end], has_side[side]))
                def _():
                    cor_copy(raw, cor, par, g, end, side).start()

    def send_sums(par, g, message):
        slots[par, g, me] = message

        def one(offset, carry):
            stat_copy(par, g, offset).start()
            return carry

        lax.fori_loop(1, peers, one, 0)

    def finish_exchange(raw, col, row, cor, par, g):
        for side in range(2):
            @pl.when(has_side[side])
            def _():
                col_copy(raw, col, par, g, side, 0, SLAB).wait_send()
                col_copy(raw, col, par, g, 1 - side, 0, SLAB).wait_recv()
        for end in range(2):
            @pl.when(has_end[end])
            def _():
                row_copy(raw, row, par, g, end).wait_send()
                row_copy(raw, row, par, g, 1 - end).wait_recv()
            for side in range(2):
                @pl.when(jnp.logical_and(has_end[end], has_side[side]))
                def _():
                    cor_copy(raw, cor, par, g, end, side).wait_send()
                    cor_copy(raw, cor, par, g, 1 - end, 1 - side).wait_recv()
        arrived = slots.at[par, g, pl.ds(0, peers - 1)]
        done = pltpu.make_async_remote_copy(arrived, arrived, stat_send.at[par, g], stat_recv.at[par, g], device_id=peer(lax.rem(me + 1, peers)), device_id_type=MESH)
        done.wait_send()
        done.wait_recv()

    def message_of(sum_one, sum_two, ones):
        both = jnp.concatenate([sum_one[0:8] + sum_one[8:SUB], sum_two[0:8] + sum_two[8:SUB]], axis=1)
        return exact_dot(both, ones)

    def half_affine(par, g, spread, norm_pair, channels):
        totals = slots[par, g, 0]
        for index in range(1, peers):
            totals = totals + slots[par, g, index]
        sums = exact_dot(totals, spread)
        inv_count = 1.0 / (count * (channels // GROUPS))
        mean = sums[:, :channels] * inv_count
        inv_std = lax.rsqrt(sums[:, channels:] * inv_count - mean * mean + GN_EPS)
        pair = norm_pair.astype(F32)
        scale = inv_std * pair[0:1]
        shift = pair[1:2] - mean * scale
        scale, shift = scale * 0.5, shift * 0.5
        return jnp.concatenate([scale, scale], axis=0), jnp.concatenate([shift, shift], axis=0)

    def activate(values, scale, shift):
        half = values.astype(F32) * scale + shift
        return half + half * jnp.tanh(half)

    def activation(raw, act, col, row, cor, par, g, scale, shift, block):
        def body(step, carry):
            first = step * block
            out = activate(raw[g, pl.ds(first, block)], scale, shift).astype(BF16)
            act[pl.ds(first + 1, block), 0:8, 1] = out[:, :, 0]
            act[pl.ds(first + 1, block), 1:9, 0] = out[:, :, 1]
            for side in range(2):
                edge = activate(col[par, g, side, pl.ds(first, block)], scale, shift)
                act[pl.ds(first + 1, block), 8 * side, side] = jnp.where(has_side[side], edge, 0.0).astype(BF16)
            return carry

        lax.fori_loop(0, SLAB // block, body, 0)
        for end in range(2):
            keep, other = (slice(8, SUB), slice(0, 8)) if end == 0 else (slice(0, 8), slice(8, SUB))
            dest = 0 if end == 0 else SLAB + 1
            inner = SLAB if end == 0 else 1

            def put(pair_at, which, remote, present):
                mine = act[inner, pair_at, which].astype(F32)
                far = jnp.where(present, remote, 0.0)[..., keep, :]
                near = mine[..., other, :]
                parts = [far, near] if end == 0 else [near, far]
                act[dest, pair_at, which] = jnp.concatenate(parts, axis=-2).astype(BF16)

            line = activate(row[par, g, end], scale, shift)
            put(slice(0, 8), 1, line[:, 0], has_end[end])
            put(slice(1, 9), 0, line[:, 1], has_end[end])
            for side in range(2):
                spot = activate(cor[par, g, end, side], scale, shift)
                put(8 * side, side, spot, jnp.logical_and(has_end[end], has_side[side]))

    def windows(act, first, channels):
        taps = []
        for row_off in range(3):
            for col_off in range(4):
                pair_at = col_off // 2
                taps.append(act[pl.ds(first + row_off, BLOCK), pair_at:pair_at + 8, col_off % 2].reshape(BLOCK * LANES, channels))
        return taps

    def convolve(act, channels, weights, bias, dst, col, row, cor, par, g, extra=None, residual=None):
        bias_pair = jnp.concatenate([bias, bias], axis=1)

        def body(step, carry):
            sum_one, sum_two = carry
            first = step * BLOCK
            taps = windows(act, first, channels)
            if extra is not None:
                taps = taps + extra(first)
            out = jnp.dot(jnp.concatenate(taps, axis=1), weights(), preferred_element_type=F32) + bias_pair
            if residual is not None:
                kept = residual[g, pl.ds(first, BLOCK)].astype(F32)
                kept = jnp.concatenate([kept[:, :, 0], kept[:, :, 1]], axis=-1)
                out = out + kept.reshape(BLOCK * LANES, WIDE)
            rounded = out.astype(BF16)
            wide = rounded.astype(F32).reshape(BLOCK * 8, SUB, WIDE)
            sum_one = sum_one + jnp.sum(wide, axis=0)
            sum_two = sum_two + jnp.sum(wide * wide, axis=0)
            tiles = rounded.reshape(BLOCK, 8, SUB, WIDE)
            dst[g, pl.ds(first, BLOCK), :, 0] = tiles[..., :LANES]
            dst[g, pl.ds(first, BLOCK), :, 1] = tiles[..., LANES:]

            @pl.when(step > 0)
            def _():
                send_cols(dst, col, par, g, step - 1)

            return sum_one, sum_two

        zero = jnp.zeros((SUB, WIDE), F32)
        sum_one, sum_two = lax.fori_loop(0, STEPS, body, (zero, zero))
        send_sums(par, g, message_of(sum_one[:, :LANES] + sum_one[:, LANES:], sum_two[:, :LANES] + sum_two[:, LANES:], sum_t[...]))
        send_cols(dst, col, par, g, STEPS - 1)
        send_ends(dst, row, cor, par, g)

    def input_copy(g, chunk, half):
        index = g * CHUNKS + chunk
        slot = lax.rem(index, DEPTH)
        src = act_in.at[pl.ds(g * 8, 8), pl.ds(half * SLAB + chunk * CHUNK, CHUNK)]
        return pltpu.make_async_copy(src, stage.at[slot, half], in_sem.at[slot, half])

    for early in range(DEPTH):
        for half in range(2):
            input_copy(0, early, half).start()

    barrier = pltpu.get_barrier_semaphore()

    def greet(offset, carry):
        pl.semaphore_signal(barrier, inc=1, device_id=peer(lax.rem(me + offset, peers)), device_id_type=MESH)
        return carry

    lax.fori_loop(1, peers, greet, 0)

    out_row = lax.broadcasted_iota(jnp.int32, (WIDE, WIDE), 0)
    in_row = lax.broadcasted_iota(jnp.int32, (WIDE, WIDE), 1)
    swapped = jnp.logical_and(out_row // SUB == in_row % SUB, out_row % SUB == in_row // SUB)
    perm[...] = jnp.where(swapped, 1.0, 0.0).astype(BF16)
    sum_a[...] = group_matrix(WIDE, False)
    sum_t[...] = group_matrix(LANES, False)
    cast_a[...] = group_matrix(WIDE, True)
    cast_t[...] = group_matrix(LANES, True)
    for tap in range(3):
        wf[tap, 3, :, 0:LANES] = jnp.zeros((WIDE, LANES), BF16)
        wf[tap, 0, :, LANES:WIDE] = jnp.zeros((WIDE, LANES), BF16)
        for layer in range(5):
            wr[layer, tap, 3, :, 0:LANES] = jnp.zeros((LANES, LANES), BF16)
            wr[layer, tap, 0, :, LANES:WIDE] = jnp.zeros((LANES, LANES), BF16)
    ws[0, :, LANES:WIDE] = jnp.zeros((WIDE, LANES), BF16)
    ws[1, :, 0:LANES] = jnp.zeros((WIDE, LANES), BF16)

    def weight_copies():
        copies = []
        for out_col in range(2):
            lanes = pl.ds(out_col * LANES, LANES)
            copies.append(pltpu.make_async_copy(w_first, wf.at[:, pl.ds(out_col, 3), :, lanes], wt_sem.at[0, out_col]))
            copies.append(pltpu.make_async_copy(w_short, ws.at[out_col, :, lanes], wt_sem.at[1, out_col]))
            copies.append(pltpu.make_async_copy(w_rest, wr.at[:, :, pl.ds(out_col, 3), :, lanes], wt_sem.at[2, out_col]))
        return copies

    for copy in weight_copies():
        copy.start()

    blank = jnp.zeros((3, LANES), F32)
    for row_off in range(3):
        for col_off in range(4):
            parts = []
            for out_col in range(2):
                tap = col_off - out_col
                parts.append(w_out[row_off, tap].astype(F32) if 0 <= tap < 3 else blank)
            parts.append(jnp.zeros((10, LANES), F32))
            at_lane = (row_off * 4 + col_off) * LANES
            wo[:, at_lane:at_lane + LANES] = jnp.concatenate(parts, axis=0).astype(BF16)

    def load_group(g, carry):
        def body(chunk, sums):
            sum_one, sum_two = sums
            index = g * CHUNKS + chunk
            slot = lax.rem(index, DEPTH)
            for half in range(2):
                input_copy(g, chunk, half).wait()
            for line in range(CHUNK):
                tile = stage[slot, :, :, line].reshape(WIDE, WIDE)
                out = jnp.dot(perm[...], tile, preferred_element_type=F32)
                cube = out.reshape(SUB, SUB, WIDE)
                sum_one = sum_one + jnp.sum(cube, axis=0)
                sum_two = sum_two + jnp.sum(cube * cube, axis=0)
                raw_a[g, chunk * CHUNK + line] = out.astype(BF16).reshape(8, 2, SUB, WIDE)
            later = index + DEPTH

            @pl.when(later < 2 * CHUNKS)
            def _():
                next_g = later // CHUNKS
                for half in range(2):
                    input_copy(next_g, later - next_g * CHUNKS, half).start()

            @pl.when(jnp.logical_and(index == 1, g == 0))
            def _():
                pl.semaphore_wait(barrier, peers - 1)

            @pl.when(jnp.logical_and(lax.rem(chunk, 2) == 0, chunk > 0))
            def _():
                send_cols(raw_a, col_a, 0, g, chunk // 2 - 1)

            return sum_one, sum_two

        zero = jnp.zeros((SUB, WIDE), F32)
        sum_one, sum_two = lax.fori_loop(0, CHUNKS, body, (zero, zero))
        send_sums(0, g, message_of(sum_one, sum_two, sum_a[...]))
        send_cols(raw_a, col_a, 0, g, STEPS - 1)
        send_ends(raw_a, row_a, cor_a, 0, g)
        return carry

    lax.fori_loop(0, 2, load_group, 0)
    for copy in weight_copies():
        copy.wait()

    def bias_row(index):
        return bias_rest[index].astype(F32)

    def first_conv(g, carry):
        finish_exchange(raw_a, col_a, row_a, cor_a, 0, g)
        scale, shift = half_affine(0, g, cast_a[...], norm_first[...], WIDE)
        activation(raw_a, act_a, col_a, row_a, cor_a, 0, g, scale, shift, 2)
        convolve(act_a, WIDE, lambda: wf[...].reshape(3072, WIDE), bias_row(0), raw_t, col_t, row_t, cor_t, 1, g)
        return carry

    lax.fori_loop(0, 2, first_conv, 0)

    def layer(src, norm_at, weights, bias, dst, par, g, **more):
        finish_exchange(src, col_t, row_t, cor_t, par, g)
        scale, shift = half_affine(par, g, cast_t[...], norm_rest[norm_at], LANES)
        activation(src, act_t, col_t, row_t, cor_t, par, g, scale, shift, 4)
        if weights is not None:
            convolve(act_t, LANES, weights, bias, dst, col_t, row_t, cor_t, 1 - par, g, **more)

    def shortcut_conv(g, carry):
        def extra(first):
            return [raw_a[g, pl.ds(first, BLOCK), :, which].reshape(BLOCK * LANES, WIDE) for which in range(2)]

        def weights():
            return jnp.concatenate([wr[0].reshape(1536, WIDE), ws[...].reshape(512, WIDE)], axis=0)

        layer(raw_t, 0, weights, bias_row(1) + bias_row(6), raw_h, 1, g, extra=extra)
        return carry

    lax.fori_loop(0, 2, shortcut_conv, 0)

    def resnet(res, carry):
        base = 2 * res + 1

        def first_half(g, inner):
            layer(raw_h, base, lambda: wr[base].reshape(1536, WIDE), bias_row(base + 1), raw_t, 0, g)
            return inner

        def second_half(g, inner):
            layer(raw_t, base + 1, lambda: wr[base + 1].reshape(1536, WIDE), bias_row(base + 2), raw_h, 1, g, residual=raw_h)
            return inner

        lax.fori_loop(0, 2, first_half, 0)
        lax.fori_loop(0, 2, second_half, 0)
        return carry

    lax.fori_loop(0, 2, resnet, 0)

    def out_conv(g, carry):
        layer(raw_h, 5, None, None, None, 0, g)

        def body(step, inner):
            taps = jnp.concatenate(windows(act_t, step * BLOCK, LANES), axis=1)
            out = lax.dot_general(wo[...], taps, (((1,), (1,)), ((), ())), preferred_element_type=F32)
            image[g, step] = out[0:8]
            return inner

        lax.fori_loop(0, STEPS, body, 0)
        return carry

    lax.fori_loop(0, 2, out_conv, 0)


def solution(mesh):
    rows_n = mesh.shape["sy"]
    cols_n = mesh.shape["sx"]
    tile_spec = P("dp", "sy", "sx", None)
    replicated = P()
    dma = pltpu.SemaphoreType.DMA

    def local_decode(act_in, norm_first, w_first, w_short, norm_rest, w_rest, bias_rest, w_out, bias_out):
        vmem = pl.BlockSpec(memory_space=pltpu.VMEM)
        anywhere = pl.BlockSpec(memory_space=pl.ANY)
        tall = pl.pallas_call(
            functools.partial(kernel, rows_n, cols_n),
            out_shape=jax.ShapeDtypeStruct((2, STEPS, 8, BLOCK * LANES), F32),
            in_specs=[anywhere, vmem, anywhere, anywhere, vmem, anywhere, vmem, vmem],
            out_specs=vmem,
            scratch_shapes=[
                pltpu.VMEM((DEPTH, 2, 8, CHUNK, SUB, WIDE), BF16),
                pltpu.VMEM((2, SLAB, 8, 2, SUB, WIDE), BF16),
                pltpu.VMEM((2, SLAB, 8, 2, SUB, LANES), BF16),
                pltpu.VMEM((2, SLAB, 8, 2, SUB, LANES), BF16),
                pltpu.VMEM((SLAB + 2, 9, 2, SUB, WIDE), BF16),
                pltpu.VMEM((SLAB + 2, 9, 2, SUB, LANES), BF16),
                pltpu.VMEM((3, 4, WIDE, WIDE), BF16),
                pltpu.VMEM((2, WIDE, WIDE), BF16),
                pltpu.VMEM((5, 3, 4, LANES, WIDE), BF16),
                pltpu.VMEM((SUB, 1536), BF16),
                pltpu.VMEM((WIDE, WIDE), BF16),
                pltpu.VMEM((512, LANES), BF16),
                pltpu.VMEM((WIDE, LANES), BF16),
                pltpu.VMEM((LANES, 512), BF16),
                pltpu.VMEM((LANES, WIDE), BF16),
                pltpu.VMEM((1, 2, 2, SLAB, SUB, WIDE), BF16),
                pltpu.VMEM((1, 2, 2, 8, 2, SUB, WIDE), BF16),
                pltpu.VMEM((1, 2, 2, 2, SUB, WIDE), BF16),
                pltpu.VMEM((2, 2, 2, SLAB, SUB, LANES), BF16),
                pltpu.VMEM((2, 2, 2, 8, 2, SUB, LANES), BF16),
                pltpu.VMEM((2, 2, 2, 2, SUB, LANES), BF16),
                pltpu.VMEM((2, 2, rows_n * cols_n, 8, LANES), F32),
                dma((DEPTH, 2)),
                dma((3, 2)),
                dma((2, 2, 2)),
                dma((2, 2, 2)),
                dma((2, 2, 2)),
                dma((2, 2, 2)),
                dma((2, 2, 2, 2)),
                dma((2, 2, 2, 2)),
                dma((2, 2)),
                dma((2, 2)),
            ],
            compiler_params=pltpu.CompilerParams(collective_id=0, has_side_effects=True, vmem_limit_bytes=62 << 20),
            name="decode",
        )(act_in, norm_first, w_first, w_short, norm_rest, w_rest, bias_rest.reshape(7, 1, LANES), jnp.transpose(w_out, (0, 1, 3, 2)))
        parts = tall[:, :, :6].reshape(2, STEPS, 2, 3, BLOCK, 8, 2, 8)
        image = jnp.transpose(parts, (0, 7, 6, 1, 4, 5, 2, 3)).reshape(SUB, 2 * SLAB, SUB, 3)
        return image + bias_out.astype(F32)

    return jax.shard_map(local_decode, mesh=mesh, in_specs=(tile_spec, replicated, replicated, replicated, replicated, replicated, replicated, replicated, replicated), out_specs=tile_spec, check_vma=False)
```

time: 861 us -> 178 us (0.21); the launches traced: 850 us -> 177 us
  blocking collectives: 416 us -> 0 us
  matrix products: 210 us -> 0 us
  Pallas kernels: 0 us -> 151 us
  waiting for transfers between devices: 96.4 us -> 0 us
  other arithmetic: 79.7 us -> 0.84 us
  starting transfers between devices: 39.8 us -> 0 us
  local copies, waits for them, and re-layouts: 6.51 us -> 25.1 us
    psum x7 -> x0, blocking collectives: 416 us -> none  [group_norm_act(): totals = lax.psum(jnp.stack([sum_one, sum_two], axis=-1), ('sy', 'sx'))]
    conv_general_dilated x7 -> x0, matrix products: 197 us -> none  [conv_tile(): lax.conv_general_dilated(add_border(act_map), kernel, (1, 1), ((0, 0), (0...]
    pallas_call x0 -> x1, Pallas kernels: none -> 151 us  [local_decode(): pl.pallas_call(functools.partial(kernel, rows_n, cols_n), out_shape=jax.S...]
    ppermute x28 -> x0, waiting for transfers between devices: 96.4 us -> none  [the longest x7 42.8 us: add_border(): left_col = lax.ppermute(tall[:, :, -1:], 'sx', to_right)]
    convert_element_type x10 -> x1, other arithmetic: 60.2 us -> 0.01 us  [local_decode(): return image + bias_out.astype(F32)]
    ppermute x28 -> x0, starting transfers between devices: 39.8 us -> none  [the longest x7 11 us: add_border(): left_col = lax.ppermute(tall[:, :, -1:], 'sx', to_right)]
    reduce_sum x15 -> x0, other arithmetic: 18.4 us -> none  [the longest x8 18.1 us: group_norm_act(): jnp.sum(act_map, axis=(1, 2), dtype=jnp.float32)]
    reshape x16 -> x3, local copies, waits for them, and re-layouts: 0.75 us -> 15.1 us  [the longest x1 9.05 us: local_decode(): parts = tall[:, :, :6].reshape(2, STEPS, 2, 3, BLOCK, 8, 2, 8)]
  transfers between devices with their start and end apart: 28 -> 0, of which waited for: 19 -> 0; matrix products, arithmetic and copies ran while one was open for 2% -> 0% of each run, Pallas kernels for 0% -> 0%
where the time goes in v1:
time: 178 us; the launch traced here: 177 us
  Pallas kernels  151 us (85%)
  local copies, waits for them, and re-layouts  25.1 us (14%)
    pallas_call x1, Pallas kernels, local_decode(): pl.pallas_call(functools.partial(kernel, rows_n, cols_n), out_shape=jax.S...  151 us
    reshape x1, local copies, waits for them, and re-layouts, local_decode(): parts = tall[:, :, :6].reshape(2, STEPS, 2, 3, BLOCK, 8, 2, 8)  9.05 us
    transpose x1, local copies, waits for them, and re-layouts, local_decode(): jnp.transpose(parts, (0, 7, 6, 1, 4, 5, 2, 3))  8.79 us
    reshape x1, local copies, waits for them, and re-layouts, local_decode(): jnp.transpose(parts, (0, 7, 6, 1, 4, 5, 2, 3))  4.75 us

profile of v1, /device:TPU:0, one launch (start us, length us, event | category | flops | bytes accessed | tf_op | source)
XLA Modules:
  0.0 177.2 jit_solution(9037785203163600827)
XLA Ops:
  0.0 1.3 copy.11.bias_rest
  1.3 151.2 %decode.1 = f32[2,6,8,1024]{3,2,1,0:T(8,128)} custom-call(bf16[16,96,16,256]{3,2,1,0:T(8,128)(2,1)} %act_in.1, bf16[2,256]{1,0:T(2,128)(2,1)} %norm_first.1, bf16[3,3,256,128]{3,2,1,0:T(8,128)(2,1)} %w_first.1, bf16[256,128]{1,0:T(8,128)(2,1)} %w_short.1, bf16[6,2,128]{2,1,0:T(2,128)(2,1)} %norm_rest.1, bf16[5,3,3,128,128]{4,3,2,1,0:T(8,128)(2,1)} %w_rest.1, ...), custom_call_target="tpu_custom_call" | custom-call | tf_op jit(solution)/shard_map/decode/pallas_call | solution.py:397
  152.5 1.2 copy.12
  153.7 9.0 %reshape.11 = f32[2,6,2,3,8,8,2,8]{7,6,5,4,0,3,2,1:T(2,128)} reshape(f32[2,6,6,1024]{3,0,2,1:T(2,128)S(1)} %copy.12) | data formatting | bytes 589824 | tf_op jit(solution)/shard_map/reshape | solution.py:439
  162.7 0.0 copy-start
  162.7 8.8 %copy.13 = f32[2,8,2,6,8,8,2,3]{4,3,2,6,5,7,1,0:T(8,128)} copy(f32[2,8,2,6,8,8,2,3]{1,2,5,4,0,7,6,3:T(2,128)} %bitcast.8) | data formatting | bytes 589824 | tf_op jit(solution)/shard_map/transpose | solution.py:440
  171.5 4.8 %reshape.12 = f32[16,96,16,3]{1,2,3,0:T(8,128)S(1)} reshape(f32[2,8,2,6,8,8,2,3]{4,3,2,6,5,7,1,0:T(8,128)} %copy.13) | data formatting | bytes 589824 | tf_op jit(solution)/shard_map/reshape | solution.py:440
  176.3 0.0 copy-done
  176.3 0.8 broadcast_add_fusion
  (1 shorter events, 0.0 us)
Async XLA Ops:
  162.7 13.6 %copy-start = (bf16[3]{0:T(256)(128)(2,1)S(1)}, bf16[3]{0:T(256)(128)(2,1)}, u32[]{:S(2)}) copy-start(bf16[3]{0:T(256)(128)(2,1)} %param.17) | copy-start | bytes 22

commit v2 on v1

--- a/solution.py
+++ b/solution.py
@@ -16,7 +16,7 @@
 SUB = 16
 BF16 = jnp.bfloat16
 SLAB = 48
-BLOCK = 8
+BLOCK = 16
 STEPS = SLAB // BLOCK
 CHUNK = 4
 DEPTH = 3
@@ -46,7 +46,7 @@
 
 
 def kernel(rows_n, cols_n, act_in, norm_first, w_first, w_short, norm_rest, w_rest, bias_rest, w_out, image,
-           stage, raw_a, raw_t, raw_h, act_a, act_t, wf, ws, wr, wo, perm, sum_a, sum_t, cast_a, cast_t,
+           flat, order, bias_f, stage, raw_a, raw_t, raw_h, act_a, act_t, wf, ws, wr, wo, perm, sum_a, sum_t, cast_a, cast_t,
            col_a, row_a, cor_a, col_t, row_t, cor_t, slots,
            in_sem, wt_sem, col_send, col_recv, row_send, row_recv, cor_send, cor_recv, stat_send, stat_recv):
     peers = rows_n * cols_n
@@ -79,11 +79,11 @@
     def stat_copy(par, g, offset):
         return pltpu.make_async_remote_copy(slots.at[par, g, me], slots.at[par, g, me], stat_send.at[par, g], stat_recv.at[par, g], device_id=peer(lax.rem(me + offset, peers)), device_id_type=MESH)
 
-    def send_cols(raw, col, par, g, step):
+    def send_cols(raw, col, par, g, start, size):
         for side in range(2):
             @pl.when(has_side[side])
             def _():
-                col_copy(raw, col, par, g, side, step * BLOCK, BLOCK).start()
+                col_copy(raw, col, par, g, side, start, size).start()
 
     def send_ends(raw, row, cor, par, g):
         for end in range(2):
@@ -210,14 +210,14 @@
 
             @pl.when(step > 0)
             def _():
-                send_cols(dst, col, par, g, step - 1)
+                send_cols(dst, col, par, g, (step - 1) * BLOCK, BLOCK)
 
             return sum_one, sum_two
 
         zero = jnp.zeros((SUB, WIDE), F32)
         sum_one, sum_two = lax.fori_loop(0, STEPS, body, (zero, zero))
         send_sums(par, g, message_of(sum_one[:, :LANES] + sum_one[:, LANES:], sum_two[:, :LANES] + sum_two[:, LANES:], sum_t[...]))
-        send_cols(dst, col, par, g, STEPS - 1)
+        send_cols(dst, col, par, g, SLAB - BLOCK, BLOCK)
         send_ends(dst, row, cor, par, g)
 
     def input_copy(g, chunk, half):
@@ -242,6 +242,13 @@
     in_row = lax.broadcasted_iota(jnp.int32, (WIDE, WIDE), 1)
     swapped = jnp.logical_and(out_row // SUB == in_row % SUB, out_row % SUB == in_row // SUB)
     perm[...] = jnp.where(swapped, 1.0, 0.0).astype(BF16)
+    shape = (LANES, 2 * WIDE)
+    target = lax.broadcasted_iota(jnp.int32, shape, 0)
+    lane = lax.broadcasted_iota(jnp.int32, shape, 1)
+    half_at, col_at, pair_at = lane // WIDE, lane // LANES % 2, lane // SUB % 8
+    wanted = jnp.logical_and(lane // 8 % 2 == half_at, target == lane % 8 * SUB + 2 * pair_at + col_at)
+    order[...] = jnp.where(wanted, 1.0, 0.0).astype(BF16)
+    bias_f[0:7] = bias_rest[...].astype(F32)
     sum_a[...] = group_matrix(WIDE, False)
     sum_t[...] = group_matrix(LANES, False)
     cast_a[...] = group_matrix(WIDE, True)
@@ -300,20 +307,20 @@
                 for half in range(2):
                     input_copy(next_g, later - next_g * CHUNKS, half).start()
 
-            @pl.when(jnp.logical_and(index == 1, g == 0))
+            @pl.when(index == 1)
             def _():
                 pl.semaphore_wait(barrier, peers - 1)
 
-            @pl.when(jnp.logical_and(lax.rem(chunk, 2) == 0, chunk > 0))
-            def _():
-                send_cols(raw_a, col_a, 0, g, chunk // 2 - 1)
+            @pl.when(chunk > 0)
+            def _():
+                send_cols(raw_a, col_a, 0, g, (chunk - 1) * CHUNK, CHUNK)
 
             return sum_one, sum_two
 
         zero = jnp.zeros((SUB, WIDE), F32)
         sum_one, sum_two = lax.fori_loop(0, CHUNKS, body, (zero, zero))
         send_sums(0, g, message_of(sum_one, sum_two, sum_a[...]))
-        send_cols(raw_a, col_a, 0, g, STEPS - 1)
+        send_cols(raw_a, col_a, 0, g, SLAB - CHUNK, CHUNK)
         send_ends(raw_a, row_a, cor_a, 0, g)
         return carry
 
@@ -322,7 +329,7 @@
         copy.wait()
 
     def bias_row(index):
-        return bias_rest[index].astype(F32)
+        return bias_f[pl.ds(index, 1)]
 
     def first_conv(g, carry):
         finish_exchange(raw_a, col_a, row_a, cor_a, 0, g)
@@ -375,10 +382,22 @@
         def body(step, inner):
             taps = jnp.concatenate(windows(act_t, step * BLOCK, LANES), axis=1)
             out = lax.dot_general(wo[...], taps, (((1,), (1,)), ((), ())), preferred_element_type=F32)
-            image[g, step] = out[0:8]
+            for line in range(BLOCK):
+                flat[pl.ds(step * BLOCK + line, 8, stride=SLAB), :] = out[0:8, line * LANES:(line + 1) * LANES]
             return inner
 
         lax.fori_loop(0, STEPS, body, 0)
+        for channel in range(3):
+            lines = [flat[pl.ds((3 * out_col + channel) * SLAB, SLAB), :] for out_col in range(2)]
+            values = jnp.concatenate(lines, axis=1)
+            total = jnp.zeros((LANES, 2 * SLAB), F32)
+            for _ in range(3):
+                term = values.astype(BF16)
+                values = values - term.astype(F32)
+                blank_half = jnp.zeros_like(term)
+                spread = jnp.concatenate([jnp.concatenate([term, blank_half], axis=1), jnp.concatenate([blank_half, term], axis=1)], axis=0)
+                total = total + lax.dot_general(order[...], spread, (((1,), (1,)), ((), ())), preferred_element_type=F32)
+            image[pl.ds(g * 8, 8), channel] = total.reshape(8, SUB, 2 * SLAB)
         return carry
 
     lax.fori_loop(0, 2, out_conv, 0)
@@ -394,12 +413,15 @@
     def local_decode(act_in, norm_first, w_first, w_short, norm_rest, w_rest, bias_rest, w_out, bias_out):
         vmem = pl.BlockSpec(memory_space=pltpu.VMEM)
         anywhere = pl.BlockSpec(memory_space=pl.ANY)
-        tall = pl.pallas_call(
+        planes = pl.pallas_call(
             functools.partial(kernel, rows_n, cols_n),
-            out_shape=jax.ShapeDtypeStruct((2, STEPS, 8, BLOCK * LANES), F32),
+            out_shape=jax.ShapeDtypeStruct((SUB, 3, SUB, 2 * SLAB), F32),
             in_specs=[anywhere, vmem, anywhere, anywhere, vmem, anywhere, vmem, vmem],
             out_specs=vmem,
             scratch_shapes=[
+                pltpu.VMEM((8 * SLAB, LANES), F32),
+                pltpu.VMEM((LANES, 2 * WIDE), BF16),
+                pltpu.VMEM((8, LANES), F32),
                 pltpu.VMEM((DEPTH, 2, 8, CHUNK, SUB, WIDE), BF16),
                 pltpu.VMEM((2, SLAB, 8, 2, SUB, WIDE), BF16),
                 pltpu.VMEM((2, SLAB, 8, 2, SUB, LANES), BF16),
@@ -435,9 +457,7 @@
             ],
             compiler_params=pltpu.CompilerParams(collective_id=0, has_side_effects=True, vmem_limit_bytes=62 << 20),
             name="decode",
-        )(act_in, norm_first, w_first, w_short, norm_rest, w_rest, bias_rest.reshape(7, 1, LANES), jnp.transpose(w_out, (0, 1, 3, 2)))
-        parts = tall[:, :, :6].reshape(2, STEPS, 2, 3, BLOCK, 8, 2, 8)
-        image = jnp.transpose(parts, (0, 7, 6, 1, 4, 5, 2, 3)).reshape(SUB, 2 * SLAB, SUB, 3)
-        return image + bias_out.astype(F32)
+        )(act_in, norm_first, w_first, w_short, norm_rest, w_rest, bias_rest, jnp.transpose(w_out, (0, 1, 3, 2)))
+        return jnp.transpose(planes, (0, 3, 2, 1)) + bias_out.astype(F32)
 
     return jax.shard_map(local_decode, mesh=mesh, in_specs=(tile_spec, replicated, replicated, replicated, replicated, replicated, replicated, replicated, replicated), out_specs=tile_spec, check_vma=False)

time: 178 us -> 151 us (0.85)
  local copies, waits for them, and re-layouts: 25.1 us -> 0 us
  Pallas kernels: 151 us -> 148 us
    reshape x3 -> x0, local copies, waits for them, and re-layouts: 15.1 us -> none  [the longest x1 9.05 us: local_decode(): parts = tall[:, :, :6].reshape(2, STEPS, 2, 3, BLOCK, 8, 2, 8)]
    transpose x1 -> x0, local copies, waits for them, and re-layouts: 8.79 us -> none  [local_decode(): jnp.transpose(parts, (0, 7, 6, 1, 4, 5, 2, 3))]
    pallas_call x1, Pallas kernels: 151 us -> 148 us  [local_decode(): pl.pallas_call(functools.partial(kernel, rows_n, cols_n), out_shape=jax.S...]
where the time goes in v2:
time: 151 us
  Pallas kernels  148 us (98%)
  other arithmetic  2.49 us (2%)
    pallas_call x1, Pallas kernels, local_decode(): pl.pallas_call(functools.partial(kernel, rows_n, cols_n), out_shape=jax.S...  148 us

profile of v2, /device:TPU:0, one launch (start us, length us, event | category | flops | bytes accessed | tf_op | source)
XLA Modules:
  0.0 150.6 jit_solution(13174692441056878810)
XLA Ops:
  0.0 0.7 convert_element_type.3
  0.7 148.1 %decode.1 = f32[16,3,16,96]{3,2,1,0:T(8,128)} custom-call(bf16[16,96,16,256]{3,2,1,0:T(8,128)(2,1)} %act_in.1, bf16[2,256]{1,0:T(2,128)(2,1)} %norm_first.1, bf16[3,3,256,128]{3,2,1,0:T(8,128)(2,1)} %w_first.1, bf16[256,128]{1,0:T(8,128)(2,1)} %w_short.1, bf16[6,2,128]{2,1,0:T(2,128)(2,1)} %norm_rest.1, bf16[5,3,3,128,128]{4,3,2,1,0:T(8,128)(2,1)} %w_rest.1, ...), custom_call_target="tpu_custom_call" | custom-call | tf_op jit(solution)/shard_map/decode/pallas_call | solution.py:416
  148.7 1.8 %add_bitcast_fusion = f32[16,96,16,3]{1,2,3,0:T(8,128)} fusion(f32[16,3,16,96]{3,2,1,0:T(8,128)} %decode.1, f32[3]{0:T(128)S(1)} %convert_element_type.3), kind=kLoop, calls=%fused_computation | loop fusion | flops 73728 | bytes 589836 | tf_op jit(solution)/shard_map/add | solution.py:461

commit v3 on v2

--- a/solution.py
+++ b/solution.py
@@ -16,10 +16,11 @@
 SUB = 16
 BF16 = jnp.bfloat16
 SLAB = 48
-BLOCK = 16
+BLOCK = 8
 STEPS = SLAB // BLOCK
+EARLY = 4
 CHUNK = 4
-DEPTH = 3
+DEPTH = 8
 CHUNKS = SLAB // CHUNK
 
 
@@ -46,10 +47,12 @@
 
 
 def kernel(rows_n, cols_n, act_in, norm_first, w_first, w_short, norm_rest, w_rest, bias_rest, w_out, image,
-           flat, order, bias_f, stage, raw_a, raw_t, raw_h, act_a, act_t, wf, ws, wr, wo, perm, sum_a, sum_t, cast_a, cast_t,
+           flat, order, bias_f, stage, raw_a, raw_t, raw_h, act_a0, act_a1, act_a2, act_t0, act_t1, act_t2, wf, ws, wr, wo, perm, sum_a, sum_t, cast_a, cast_t,
            col_a, row_a, cor_a, col_t, row_t, cor_t, slots,
            in_sem, wt_sem, col_send, col_recv, row_send, row_recv, cor_send, cor_recv, stat_send, stat_recv):
     peers = rows_n * cols_n
+    act_a = (act_a0, act_a1, act_a2)
+    act_t = (act_t0, act_t1, act_t2)
     my_x = lax.axis_index("sx")
     my_y = lax.axis_index("sy")
     me = my_x * rows_n + my_y
@@ -147,57 +150,71 @@
         half = values.astype(F32) * scale + shift
         return half + half * jnp.tanh(half)
 
-    def activation(raw, act, col, row, cor, par, g, scale, shift, block):
-        def body(step, carry):
-            first = step * block
-            out = activate(raw[g, pl.ds(first, block)], scale, shift).astype(BF16)
-            act[pl.ds(first + 1, block), 0:8, 1] = out[:, :, 0]
-            act[pl.ds(first + 1, block), 1:9, 0] = out[:, :, 1]
+    def activation(raw, act, col, row, cor, par, g, scale, shift):
+        def rows(ring, local, first, size):
+            out = activate(raw[g, first:first + size], scale, shift).astype(BF16)
+            ring[local:local + size, 0:8, 1] = out[:, :, 0]
+            ring[local:local + size, 1:9, 0] = out[:, :, 1]
             for side in range(2):
-                edge = activate(col[par, g, side, pl.ds(first, block)], scale, shift)
-                act[pl.ds(first + 1, block), 8 * side, side] = jnp.where(has_side[side], edge, 0.0).astype(BF16)
-            return carry
-
-        lax.fori_loop(0, SLAB // block, body, 0)
-        for end in range(2):
-            keep, other = (slice(8, SUB), slice(0, 8)) if end == 0 else (slice(0, 8), slice(8, SUB))
-            dest = 0 if end == 0 else SLAB + 1
-            inner = SLAB if end == 0 else 1
-
-            def put(pair_at, which, remote, present):
-                mine = act[inner, pair_at, which].astype(F32)
-                far = jnp.where(present, remote, 0.0)[..., keep, :]
-                near = mine[..., other, :]
-                parts = [far, near] if end == 0 else [near, far]
-                act[dest, pair_at, which] = jnp.concatenate(parts, axis=-2).astype(BF16)
-
-            line = activate(row[par, g, end], scale, shift)
-            put(slice(0, 8), 1, line[:, 0], has_end[end])
-            put(slice(1, 9), 0, line[:, 1], has_end[end])
+                edge = activate(col[par, g, side, first:first + size], scale, shift)
+                ring[local:local + size, 8 * side, side] = jnp.where(has_side[side], edge, 0.0).astype(BF16)
+
+        def outer_row(ring, local, end):
+            inner = SLAB - 1 if end == 0 else 0
+            low, high = slice(0, 8), slice(8, SUB)
+            own, far = (low, high) if end == 0 else (high, low)
+
+            def join(mine, theirs, mine_present, theirs_present):
+                near = activate(mine.astype(F32)[..., own, :], scale[0:8], shift[0:8])
+                away = activate(theirs.astype(F32)[..., far, :], scale[0:8], shift[0:8])
+                if mine_present is not None:
+                    near = jnp.where(mine_present, near, 0.0)
+                away = jnp.where(theirs_present, away, 0.0)
+                return jnp.concatenate([away, near] if end == 0 else [near, away], axis=-2).astype(BF16)
+
+            line = join(raw[g, inner], row[par, g, end], None, has_end[end])
+            ring[local, 0:8, 1] = line[:, 0]
+            ring[local, 1:9, 0] = line[:, 1]
             for side in range(2):
-                spot = activate(cor[par, g, end, side], scale, shift)
-                put(8 * side, side, spot, jnp.logical_and(has_end[end], has_side[side]))
-
-    def windows(act, first, channels):
-        taps = []
-        for row_off in range(3):
-            for col_off in range(4):
-                pair_at = col_off // 2
-                taps.append(act[pl.ds(first + row_off, BLOCK), pair_at:pair_at + 8, col_off % 2].reshape(BLOCK * LANES, channels))
-        return taps
-
-    def convolve(act, channels, weights, bias, dst, col, row, cor, par, g, extra=None, residual=None):
+                both = jnp.logical_and(has_end[end], has_side[side])
+                ring[local, 8 * side, side] = join(col[par, g, side, inner], cor[par, g, end, side], has_side[side], both)
+
+        def chunk(index):
+            ring = act[index % 3]
+            if index < 0:
+                outer_row(ring, BLOCK - 2, 0)
+                rows(ring, BLOCK - 1, 0, 1)
+            elif index < STEPS - 1:
+                rows(ring, 0, index * BLOCK + 1, BLOCK)
+            elif index == STEPS - 1:
+                rows(ring, 0, index * BLOCK + 1, BLOCK - 1)
+                outer_row(ring, BLOCK - 1, 1)
+
+        return chunk
+
+    def window(act, index, row_off, col_off, channels):
+        pair_at = slice(col_off // 2, col_off // 2 + 8)
+        which = col_off % 2
+        low = row_off - 2
+        if low == 0:
+            out = act[index % 3][:, pair_at, which]
+        else:
+            out = jnp.concatenate([act[(index - 1) % 3][BLOCK + low:BLOCK, pair_at, which], act[index % 3][0:BLOCK + low, pair_at, which]], axis=0)
+        return out.reshape(BLOCK * LANES, channels)
+
+    def convolve(act, chunk, channels, weights, bias, dst, col, row, cor, par, g, extra=None, residual=None):
         bias_pair = jnp.concatenate([bias, bias], axis=1)
-
-        def body(step, carry):
-            sum_one, sum_two = carry
-            first = step * BLOCK
-            taps = windows(act, first, channels)
+        sum_one = sum_two = jnp.zeros((SUB, WIDE), F32)
+        chunk(-1)
+        chunk(0)
+        for step in range(STEPS):
+            span = slice(step * BLOCK, step * BLOCK + BLOCK)
+            taps = [window(act, step, row_off, col_off, channels) for row_off in range(3) for col_off in range(4)]
             if extra is not None:
-                taps = taps + extra(first)
+                taps = taps + extra(span)
             out = jnp.dot(jnp.concatenate(taps, axis=1), weights(), preferred_element_type=F32) + bias_pair
             if residual is not None:
-                kept = residual[g, pl.ds(first, BLOCK)].astype(F32)
+                kept = residual[g, span].astype(F32)
                 kept = jnp.concatenate([kept[:, :, 0], kept[:, :, 1]], axis=-1)
                 out = out + kept.reshape(BLOCK * LANES, WIDE)
             rounded = out.astype(BF16)
@@ -205,20 +222,14 @@
             sum_one = sum_one + jnp.sum(wide, axis=0)
             sum_two = sum_two + jnp.sum(wide * wide, axis=0)
             tiles = rounded.reshape(BLOCK, 8, SUB, WIDE)
-            dst[g, pl.ds(first, BLOCK), :, 0] = tiles[..., :LANES]
-            dst[g, pl.ds(first, BLOCK), :, 1] = tiles[..., LANES:]
-
-            @pl.when(step > 0)
-            def _():
-                send_cols(dst, col, par, g, (step - 1) * BLOCK, BLOCK)
-
-            return sum_one, sum_two
-
-        zero = jnp.zeros((SUB, WIDE), F32)
-        sum_one, sum_two = lax.fori_loop(0, STEPS, body, (zero, zero))
+            dst[g, span, :, 0] = tiles[..., :LANES]
+            dst[g, span, :, 1] = tiles[..., LANES:]
+            chunk(step + 1)
+            if step == EARLY - 1:
+                send_cols(dst, col, par, g, 0, EARLY * BLOCK)
         send_sums(par, g, message_of(sum_one[:, :LANES] + sum_one[:, LANES:], sum_two[:, :LANES] + sum_two[:, LANES:], sum_t[...]))
-        send_cols(dst, col, par, g, SLAB - BLOCK, BLOCK)
         send_ends(dst, row, cor, par, g)
+        send_cols(dst, col, par, g, EARLY * BLOCK, SLAB - EARLY * BLOCK)
 
     def input_copy(g, chunk, half):
         index = g * CHUNKS + chunk
@@ -262,28 +273,30 @@
     ws[0, :, LANES:WIDE] = jnp.zeros((WIDE, LANES), BF16)
     ws[1, :, 0:LANES] = jnp.zeros((WIDE, LANES), BF16)
 
-    def weight_copies():
+    def weight_copies(first):
         copies = []
         for out_col in range(2):
             lanes = pl.ds(out_col * LANES, LANES)
-            copies.append(pltpu.make_async_copy(w_first, wf.at[:, pl.ds(out_col, 3), :, lanes], wt_sem.at[0, out_col]))
-            copies.append(pltpu.make_async_copy(w_short, ws.at[out_col, :, lanes], wt_sem.at[1, out_col]))
-            copies.append(pltpu.make_async_copy(w_rest, wr.at[:, :, pl.ds(out_col, 3), :, lanes], wt_sem.at[2, out_col]))
+            if first:
+                copies.append(pltpu.make_async_copy(w_first, wf.at[:, pl.ds(out_col, 3), :, lanes], wt_sem.at[0, out_col]))
+            else:
+                copies.append(pltpu.make_async_copy(w_short, ws.at[out_col, :, lanes], wt_sem.at[1, out_col]))
+                copies.append(pltpu.make_async_copy(w_rest, wr.at[:, :, pl.ds(out_col, 3), :, lanes], wt_sem.at[2, out_col]))
         return copies
 
-    for copy in weight_copies():
+    for copy in weight_copies(True):
         copy.start()
 
     blank = jnp.zeros((3, LANES), F32)
+    blocks = []
     for row_off in range(3):
+        parts = []
         for col_off in range(4):
-            parts = []
-            for out_col in range(2):
-                tap = col_off - out_col
-                parts.append(w_out[row_off, tap].astype(F32) if 0 <= tap < 3 else blank)
-            parts.append(jnp.zeros((10, LANES), F32))
-            at_lane = (row_off * 4 + col_off) * LANES
-            wo[:, at_lane:at_lane + LANES] = jnp.concatenate(parts, axis=0).astype(BF16)
+            taps = [w_out[row_off, col_off - out_col].astype(F32) if 0 <= col_off - out_col < 3 else blank for out_col in range(2)]
+            parts.append(jnp.concatenate(taps + [blank[0:2]], axis=0))
+        blocks.append(jnp.concatenate(parts, axis=1))
+    blocks.append(jnp.zeros_like(blocks[0]))
+    wo[...] = jnp.concatenate(blocks, axis=0).astype(BF16)
 
     def load_group(g, carry):
         def body(chunk, sums):
@@ -325,7 +338,9 @@
         return carry
 
     lax.fori_loop(0, 2, load_group, 0)
-    for copy in weight_copies():
+    for copy in weight_copies(False):
+        copy.start()
+    for copy in weight_copies(True):
         copy.wait()
 
     def bias_row(index):
@@ -334,22 +349,25 @@
     def first_conv(g, carry):
         finish_exchange(raw_a, col_a, row_a, cor_a, 0, g)
         scale, shift = half_affine(0, g, cast_a[...], norm_first[...], WIDE)
-        activation(raw_a, act_a, col_a, row_a, cor_a, 0, g, scale, shift, 2)
-        convolve(act_a, WIDE, lambda: wf[...].reshape(3072, WIDE), bias_row(0), raw_t, col_t, row_t, cor_t, 1, g)
+        chunk = activation(raw_a, act_a, col_a, row_a, cor_a, 0, g, scale, shift)
+        convolve(act_a, chunk, WIDE, lambda: wf[...].reshape(3072, WIDE), bias_row(0), raw_t, col_t, row_t, cor_t, 1, g)
         return carry
 
     lax.fori_loop(0, 2, first_conv, 0)
+    for copy in weight_copies(False):
+        copy.wait()
 
     def layer(src, norm_at, weights, bias, dst, par, g, **more):
         finish_exchange(src, col_t, row_t, cor_t, par, g)
         scale, shift = half_affine(par, g, cast_t[...], norm_rest[norm_at], LANES)
-        activation(src, act_t, col_t, row_t, cor_t, par, g, scale, shift, 4)
+        chunk = activation(src, act_t, col_t, row_t, cor_t, par, g, scale, shift)
         if weights is not None:
-            convolve(act_t, LANES, weights, bias, dst, col_t, row_t, cor_t, 1 - par, g, **more)
+            convolve(act_t, chunk, LANES, weights, bias, dst, col_t, row_t, cor_t, 1 - par, g, **more)
+        return chunk
 
     def shortcut_conv(g, carry):
-        def extra(first):
-            return [raw_a[g, pl.ds(first, BLOCK), :, which].reshape(BLOCK * LANES, WIDE) for which in range(2)]
+        def extra(span):
+            return [raw_a[g, span, :, which].reshape(BLOCK * LANES, WIDE) for which in range(2)]
 
         def weights():
             return jnp.concatenate([wr[0].reshape(1536, WIDE), ws[...].reshape(512, WIDE)], axis=0)
@@ -377,16 +395,23 @@
     lax.fori_loop(0, 2, resnet, 0)
 
     def out_conv(g, carry):
-        layer(raw_h, 5, None, None, None, 0, g)
-
-        def body(step, inner):
-            taps = jnp.concatenate(windows(act_t, step * BLOCK, LANES), axis=1)
-            out = lax.dot_general(wo[...], taps, (((1,), (1,)), ((), ())), preferred_element_type=F32)
-            for line in range(BLOCK):
-                flat[pl.ds(step * BLOCK + line, 8, stride=SLAB), :] = out[0:8, line * LANES:(line + 1) * LANES]
-            return inner
-
-        lax.fori_loop(0, STEPS, body, 0)
+        chunk = layer(raw_h, 5, None, None, None, 0, g)
+        sums = {}
+
+        def products(ring, local, first):
+            taps = [ring[local:BLOCK, col_off // 2:col_off // 2 + 8, col_off % 2].reshape((BLOCK - local) * LANES, LANES) for col_off in range(4)]
+            out = lax.dot_general(wo[...], jnp.concatenate(taps, axis=1), (((1,), (1,)), ((), ())), preferred_element_type=F32)
+            for line in range(BLOCK - local):
+                sums[first + line] = out[:, line * LANES:(line + 1) * LANES]
+
+        chunk(-1)
+        products(act_t[2], BLOCK - 2, 0)
+        chunk(0)
+        for step in range(STEPS):
+            chunk(step + 1)
+            products(act_t[step % 3], 0, step * BLOCK + 2)
+            for line in range(step * BLOCK, step * BLOCK + BLOCK):
+                flat[pl.ds(line, 8, stride=SLAB), :] = sums[line][0:8] + sums[line + 1][8:SUB] + sums[line + 2][SUB:SUB + 8]
         for channel in range(3):
             lines = [flat[pl.ds((3 * out_col + channel) * SLAB, SLAB), :] for out_col in range(2)]
             values = jnp.concatenate(lines, axis=1)
@@ -426,12 +451,12 @@
                 pltpu.VMEM((2, SLAB, 8, 2, SUB, WIDE), BF16),
                 pltpu.VMEM((2, SLAB, 8, 2, SUB, LANES), BF16),
                 pltpu.VMEM((2, SLAB, 8, 2, SUB, LANES), BF16),
-                pltpu.VMEM((SLAB + 2, 9, 2, SUB, WIDE), BF16),
-                pltpu.VMEM((SLAB + 2, 9, 2, SUB, LANES), BF16),
+                *[pltpu.VMEM((BLOCK, 9, 2, SUB, WIDE), BF16)] * 3,
+                *[pltpu.VMEM((BLOCK, 9, 2, SUB, LANES), BF16)] * 3,
                 pltpu.VMEM((3, 4, WIDE, WIDE), BF16),
                 pltpu.VMEM((2, WIDE, WIDE), BF16),
                 pltpu.VMEM((5, 3, 4, LANES, WIDE), BF16),
-                pltpu.VMEM((SUB, 1536), BF16),
+                pltpu.VMEM((32, 4 * LANES), BF16),
                 pltpu.VMEM((WIDE, WIDE), BF16),
                 pltpu.VMEM((512, LANES), BF16),
                 pltpu.VMEM((WIDE, LANES), BF16),

time: 151 us -> 129 us (0.85)
  Pallas kernels: 148 us -> 126 us
    pallas_call x1, Pallas kernels: 148 us -> 126 us  [local_decode(): pl.pallas_call(functools.partial(kernel, rows_n, cols_n), out_shape=jax.S...]
where the time goes in v3:
time: 129 us
  Pallas kernels  126 us (98%)
  other arithmetic  2.49 us (2%)
    pallas_call x1, Pallas kernels, local_decode(): pl.pallas_call(functools.partial(kernel, rows_n, cols_n), out_shape=jax.S...  126 us

profile of v3, /device:TPU:0, one launch (start us, length us, event | category | flops | bytes accessed | tf_op | source)
XLA Modules:
  0.0 128.7 jit_solution(3642880654482235620)
XLA Ops:
  0.0 0.7 convert_element_type.3
  0.7 126.2 %decode.1 = f32[16,3,16,96]{3,2,1,0:T(8,128)} custom-call(bf16[16,96,16,256]{3,2,1,0:T(8,128)(2,1)} %act_in.1, bf16[2,256]{1,0:T(2,128)(2,1)} %norm_first.1, bf16[3,3,256,128]{3,2,1,0:T(8,128)(2,1)} %w_first.1, bf16[256,128]{1,0:T(8,128)(2,1)} %w_short.1, bf16[6,2,128]{2,1,0:T(2,128)(2,1)} %norm_rest.1, bf16[5,3,3,128,128]{4,3,2,1,0:T(8,128)(2,1)} %w_rest.1, ...), custom_call_target="tpu_custom_call" | custom-call | tf_op jit(solution)/shard_map/decode/pallas_call | solution.py:441
  126.8 1.8 %add_bitcast_fusion = f32[16,96,16,3]{1,2,3,0:T(8,128)} fusion(f32[16,3,16,96]{3,2,1,0:T(8,128)} %decode.1, f32[3]{0:T(128)S(1)} %convert_element_type.3), kind=kLoop, calls=%fused_computation | loop fusion | flops 73728 | bytes 589836 | tf_op jit(solution)/shard_map/add | solution.py:486

commit v4 on v3

--- a/solution.py
+++ b/solution.py
@@ -14,6 +14,9 @@
 LANES = 128
 WIDE = 256
 SUB = 16
+SIDE = 512
+DEEP = 1024
+PAIR = (0, 1)
 BF16 = jnp.bfloat16
 SLAB = 48
 BLOCK = 8
@@ -47,7 +50,7 @@
 
 
 def kernel(rows_n, cols_n, act_in, norm_first, w_first, w_short, norm_rest, w_rest, bias_rest, w_out, image,
-           flat, order, bias_f, stage, raw_a, raw_t, raw_h, act_a0, act_a1, act_a2, act_t0, act_t1, act_t2, wf, ws, wr, wo, perm, sum_a, sum_t, cast_a, cast_t,
+           flat, order, bias_f, stage, raw_a, raw_t, raw_h, act_a0, act_a1, act_a2, act_t0, act_t1, act_t2, wf, wfs, ws, wr, wrs, wo, perm, sum_a, sum_t, cast_a, cast_t,
            col_a, row_a, cor_a, col_t, row_t, cor_t, slots,
            in_sem, wt_sem, col_send, col_recv, row_send, row_recv, cor_send, cor_recv, stat_send, stat_recv):
     peers = rows_n * cols_n
@@ -83,17 +86,17 @@
         return pltpu.make_async_remote_copy(slots.at[par, g, me], slots.at[par, g, me], stat_send.at[par, g], stat_recv.at[par, g], device_id=peer(lax.rem(me + offset, peers)), device_id_type=MESH)
 
     def send_cols(raw, col, par, g, start, size):
-        for side in range(2):
+        for side in PAIR:
             @pl.when(has_side[side])
             def _():
                 col_copy(raw, col, par, g, side, start, size).start()
 
     def send_ends(raw, row, cor, par, g):
-        for end in range(2):
+        for end in PAIR:
             @pl.when(has_end[end])
             def _():
                 row_copy(raw, row, par, g, end).start()
-            for side in range(2):
+            for side in PAIR:
                 @pl.when(jnp.logical_and(has_end[end], has_side[side]))
                 def _():
                     cor_copy(raw, cor, par, g, end, side).start()
@@ -108,17 +111,17 @@
         lax.fori_loop(1, peers, one, 0)
 
     def finish_exchange(raw, col, row, cor, par, g):
-        for side in range(2):
+        for side in PAIR:
             @pl.when(has_side[side])
             def _():
                 col_copy(raw, col, par, g, side, 0, SLAB).wait_send()
                 col_copy(raw, col, par, g, 1 - side, 0, SLAB).wait_recv()
-        for end in range(2):
+        for end in PAIR:
             @pl.when(has_end[end])
             def _():
                 row_copy(raw, row, par, g, end).wait_send()
                 row_copy(raw, row, par, g, 1 - end).wait_recv()
-            for side in range(2):
+            for side in PAIR:
                 @pl.when(jnp.logical_and(has_end[end], has_side[side]))
                 def _():
                     cor_copy(raw, cor, par, g, end, side).wait_send()
@@ -155,7 +158,7 @@
             out = activate(raw[g, first:first + size], scale, shift).astype(BF16)
             ring[local:local + size, 0:8, 1] = out[:, :, 0]
             ring[local:local + size, 1:9, 0] = out[:, :, 1]
-            for side in range(2):
+            for side in PAIR:
                 edge = activate(col[par, g, side, first:first + size], scale, shift)
                 ring[local:local + size, 8 * side, side] = jnp.where(has_side[side], edge, 0.0).astype(BF16)
 
@@ -175,7 +178,7 @@
             line = join(raw[g, inner], row[par, g, end], None, has_end[end])
             ring[local, 0:8, 1] = line[:, 0]
             ring[local, 1:9, 0] = line[:, 1]
-            for side in range(2):
+            for side in PAIR:
                 both = jnp.logical_and(has_end[end], has_side[side])
                 ring[local, 8 * side, side] = join(col[par, g, side, inner], cor[par, g, end, side], has_side[side], both)
 
@@ -192,15 +195,18 @@
 
         return chunk
 
-    def window(act, index, row_off, col_off, channels):
-        pair_at = slice(col_off // 2, col_off // 2 + 8)
-        which = col_off % 2
-        low = row_off - 2
-        if low == 0:
-            out = act[index % 3][:, pair_at, which]
-        else:
-            out = jnp.concatenate([act[(index - 1) % 3][BLOCK + low:BLOCK, pair_at, which], act[index % 3][0:BLOCK + low, pair_at, which]], axis=0)
-        return out.reshape(BLOCK * LANES, channels)
+    def line_of(act, index, place, col_off):
+        ring, local = (act[index % 3], place - 2) if place >= 2 else (act[(index - 1) % 3], place + BLOCK - 2)
+        return ring[local, col_off // 2:col_off // 2 + 8, col_off % 2]
+
+    def windows(act, index, places, col_off, channels):
+        lines = [line_of(act, index, place, col_off).reshape(LANES, channels) for place in places]
+        return jnp.concatenate(lines, axis=0)
+
+    def side_product(act, index, col_off, channels, weights):
+        taps = [windows(act, index, range(place, place + BLOCK, 2), col_off, channels) for place in range(4)]
+        out = jnp.dot(jnp.concatenate(taps, axis=1), weights, preferred_element_type=F32).reshape(BLOCK // 2, LANES, WIDE)
+        return jnp.stack([out[..., :LANES], out[..., LANES:]], axis=1).reshape(BLOCK * LANES, LANES)
 
     def convolve(act, chunk, channels, weights, bias, dst, col, row, cor, par, g, extra=None, residual=None):
         bias_pair = jnp.concatenate([bias, bias], axis=1)
@@ -209,10 +215,13 @@
         chunk(0)
         for step in range(STEPS):
             span = slice(step * BLOCK, step * BLOCK + BLOCK)
-            taps = [window(act, step, row_off, col_off, channels) for row_off in range(3) for col_off in range(4)]
+            taps = [windows(act, step, range(row_off, row_off + BLOCK), col_off, channels) for row_off in range(3) for col_off in (1, 2)]
             if extra is not None:
                 taps = taps + extra(span)
-            out = jnp.dot(jnp.concatenate(taps, axis=1), weights(), preferred_element_type=F32) + bias_pair
+            middle, left, right = weights()
+            sides = [side_product(act, step, 0, channels, left), side_product(act, step, 3, channels, right)]
+            out = jnp.dot(jnp.concatenate(taps, axis=1), middle, preferred_element_type=F32) + bias_pair
+            out = out + jnp.concatenate(sides, axis=1)
             if residual is not None:
                 kept = residual[g, span].astype(F32)
                 kept = jnp.concatenate([kept[:, :, 0], kept[:, :, 1]], axis=-1)
@@ -238,7 +247,7 @@
         return pltpu.make_async_copy(src, stage.at[slot, half], in_sem.at[slot, half])
 
     for early in range(DEPTH):
-        for half in range(2):
+        for half in PAIR:
             input_copy(0, early, half).start()
 
     barrier = pltpu.get_barrier_semaphore()
@@ -264,24 +273,31 @@
     sum_t[...] = group_matrix(LANES, False)
     cast_a[...] = group_matrix(WIDE, True)
     cast_t[...] = group_matrix(LANES, True)
-    for tap in range(3):
-        wf[tap, 3, :, 0:LANES] = jnp.zeros((WIDE, LANES), BF16)
-        wf[tap, 0, :, LANES:WIDE] = jnp.zeros((WIDE, LANES), BF16)
-        for layer in range(5):
-            wr[layer, tap, 3, :, 0:LANES] = jnp.zeros((LANES, LANES), BF16)
-            wr[layer, tap, 0, :, LANES:WIDE] = jnp.zeros((LANES, LANES), BF16)
+    for side in PAIR:
+        wfs[side, 3, :, 0:LANES] = jnp.zeros((WIDE, LANES), BF16)
+        wfs[side, 0, :, LANES:WIDE] = jnp.zeros((WIDE, LANES), BF16)
+        for index in range(5):
+            wrs[index, side, 3, :, 0:LANES] = jnp.zeros((LANES, LANES), BF16)
+            wrs[index, side, 0, :, LANES:WIDE] = jnp.zeros((LANES, LANES), BF16)
     ws[0, :, LANES:WIDE] = jnp.zeros((WIDE, LANES), BF16)
     ws[1, :, 0:LANES] = jnp.zeros((WIDE, LANES), BF16)
 
     def weight_copies(first):
         copies = []
-        for out_col in range(2):
+        for out_col in PAIR:
             lanes = pl.ds(out_col * LANES, LANES)
+            inner = pl.ds(1 - out_col, 2)
+            rows_at = pl.ds(out_col, 3)
             if first:
-                copies.append(pltpu.make_async_copy(w_first, wf.at[:, pl.ds(out_col, 3), :, lanes], wt_sem.at[0, out_col]))
+                copies.append(pltpu.make_async_copy(w_first.at[:, inner], wf.at[:, :, :, lanes], wt_sem.at[0, out_col, 0]))
             else:
-                copies.append(pltpu.make_async_copy(w_short, ws.at[out_col, :, lanes], wt_sem.at[1, out_col]))
-                copies.append(pltpu.make_async_copy(w_rest, wr.at[:, :, pl.ds(out_col, 3), :, lanes], wt_sem.at[2, out_col]))
+                copies.append(pltpu.make_async_copy(w_short, ws.at[out_col, :, lanes], wt_sem.at[1, out_col, 0]))
+                copies.append(pltpu.make_async_copy(w_rest.at[:, :, inner], wr.at[:, :, :, :, lanes], wt_sem.at[2, out_col, 0]))
+            for side in PAIR:
+                if first:
+                    copies.append(pltpu.make_async_copy(w_first.at[:, 2 * side], wfs.at[side, rows_at, :, lanes], wt_sem.at[0, out_col, 1 + side]))
+                else:
+                    copies.append(pltpu.make_async_copy(w_rest.at[:, :, 2 * side], wrs.at[:, side, rows_at, :, lanes], wt_sem.at[2, out_col, 1 + side]))
         return copies
 
     for copy in weight_copies(True):
@@ -292,7 +308,7 @@
     for row_off in range(3):
         parts = []
         for col_off in range(4):
-            taps = [w_out[row_off, col_off - out_col].astype(F32) if 0 <= col_off - out_col < 3 else blank for out_col in range(2)]
+            taps = [w_out[row_off, col_off - out_col].astype(F32) if 0 <= col_off - out_col < 3 else blank for out_col in PAIR]
             parts.append(jnp.concatenate(taps + [blank[0:2]], axis=0))
         blocks.append(jnp.concatenate(parts, axis=1))
     blocks.append(jnp.zeros_like(blocks[0]))
@@ -303,7 +319,7 @@
             sum_one, sum_two = sums
             index = g * CHUNKS + chunk
             slot = lax.rem(index, DEPTH)
-            for half in range(2):
+            for half in PAIR:
                 input_copy(g, chunk, half).wait()
             for line in range(CHUNK):
                 tile = stage[slot, :, :, line].reshape(WIDE, WIDE)
@@ -317,7 +333,7 @@
             @pl.when(later < 2 * CHUNKS)
             def _():
                 next_g = later // CHUNKS
-                for half in range(2):
+                for half in PAIR:
                     input_copy(next_g, later - next_g * CHUNKS, half).start()
 
             @pl.when(index == 1)
@@ -350,7 +366,7 @@
         finish_exchange(raw_a, col_a, row_a, cor_a, 0, g)
         scale, shift = half_affine(0, g, cast_a[...], norm_first[...], WIDE)
         chunk = activation(raw_a, act_a, col_a, row_a, cor_a, 0, g, scale, shift)
-        convolve(act_a, chunk, WIDE, lambda: wf[...].reshape(3072, WIDE), bias_row(0), raw_t, col_t, row_t, cor_t, 1, g)
+        convolve(act_a, chunk, WIDE, lambda: (wf[...].reshape(1536, WIDE), wfs[0].reshape(DEEP, WIDE), wfs[1].reshape(DEEP, WIDE)), bias_row(0), raw_t, col_t, row_t, cor_t, 1, g)
         return carry
 
     lax.fori_loop(0, 2, first_conv, 0)
@@ -365,12 +381,15 @@
             convolve(act_t, chunk, LANES, weights, bias, dst, col_t, row_t, cor_t, 1 - par, g, **more)
         return chunk
 
+    def side_weights(index):
+        return wrs[index, 0].reshape(SIDE, WIDE), wrs[index, 1].reshape(SIDE, WIDE)
+
     def shortcut_conv(g, carry):
         def extra(span):
             return [raw_a[g, span, :, which].reshape(BLOCK * LANES, WIDE) for which in range(2)]
 
         def weights():
-            return jnp.concatenate([wr[0].reshape(1536, WIDE), ws[...].reshape(512, WIDE)], axis=0)
+            return (jnp.concatenate([wr[0].reshape(768, WIDE), ws[...].reshape(SIDE, WIDE)], axis=0), *side_weights(0))
 
         layer(raw_t, 0, weights, bias_row(1) + bias_row(6), raw_h, 1, g, extra=extra)
         return carry
@@ -381,11 +400,11 @@
         base = 2 * res + 1
 
         def first_half(g, inner):
-            layer(raw_h, base, lambda: wr[base].reshape(1536, WIDE), bias_row(base + 1), raw_t, 0, g)
+            layer(raw_h, base, lambda: (wr[base].reshape(768, WIDE), *side_weights(base)), bias_row(base + 1), raw_t, 0, g)
             return inner
 
         def second_half(g, inner):
-            layer(raw_t, base + 1, lambda: wr[base + 1].reshape(1536, WIDE), bias_row(base + 2), raw_h, 1, g, residual=raw_h)
+            layer(raw_t, base + 1, lambda: (wr[base + 1].reshape(768, WIDE), *side_weights(base + 1)), bias_row(base + 2), raw_h, 1, g, residual=raw_h)
             return inner
 
         lax.fori_loop(0, 2, first_half, 0)
@@ -413,7 +432,7 @@
             for line in range(step * BLOCK, step * BLOCK + BLOCK):
                 flat[pl.ds(line, 8, stride=SLAB), :] = sums[line][0:8] + sums[line + 1][8:SUB] + sums[line + 2][SUB:SUB + 8]
         for channel in range(3):
-            lines = [flat[pl.ds((3 * out_col + channel) * SLAB, SLAB), :] for out_col in range(2)]
+            lines = [flat[pl.ds((3 * out_col + channel) * SLAB, SLAB), :] for out_col in PAIR]
             values = jnp.concatenate(lines, axis=1)
             total = jnp.zeros((LANES, 2 * SLAB), F32)
             for _ in range(3):
@@ -453,14 +472,16 @@
                 pltpu.VMEM((2, SLAB, 8, 2, SUB, LANES), BF16),
                 *[pltpu.VMEM((BLOCK, 9, 2, SUB, WIDE), BF16)] * 3,
                 *[pltpu.VMEM((BLOCK, 9, 2, SUB, LANES), BF16)] * 3,
-                pltpu.VMEM((3, 4, WIDE, WIDE), BF16),
+                pltpu.VMEM((3, 2, WIDE, WIDE), BF16),
+                pltpu.VMEM((2, 4, WIDE, WIDE), BF16),
                 pltpu.VMEM((2, WIDE, WIDE), BF16),
-                pltpu.VMEM((5, 3, 4, LANES, WIDE), BF16),
+                pltpu.VMEM((5, 3, 2, LANES, WIDE), BF16),
+                pltpu.VMEM((5, 2, 4, LANES, WIDE), BF16),
                 pltpu.VMEM((32, 4 * LANES), BF16),
                 pltpu.VMEM((WIDE, WIDE), BF16),
-                pltpu.VMEM((512, LANES), BF16),
+                pltpu.VMEM((SIDE, LANES), BF16),
                 pltpu.VMEM((WIDE, LANES), BF16),
-                pltpu.VMEM((LANES, 512), BF16),
+                pltpu.VMEM((LANES, SIDE), BF16),
                 pltpu.VMEM((LANES, WIDE), BF16),
                 pltpu.VMEM((1, 2, 2, SLAB, SUB, WIDE), BF16),
                 pltpu.VMEM((1, 2, 2, 8, 2, SUB, WIDE), BF16),
@@ -470,7 +491,7 @@
                 pltpu.VMEM((2, 2, 2, 2, SUB, LANES), BF16),
                 pltpu.VMEM((2, 2, rows_n * cols_n, 8, LANES), F32),
                 dma((DEPTH, 2)),
-                dma((3, 2)),
+                dma((3, 2, 3)),
                 dma((2, 2, 2)),
                 dma((2, 2, 2)),
                 dma((2, 2, 2)),

time: 129 us -> 117 us (0.907)
  Pallas kernels: 126 us -> 114 us
    pallas_call x1, Pallas kernels: 126 us -> 114 us  [local_decode(): pl.pallas_call(functools.partial(kernel, rows_n, cols_n), out_shape=jax.S...]
where the time goes in v4:
time: 117 us
  Pallas kernels  114 us (97%)
  other arithmetic  2.49 us (2%)
    pallas_call x1, Pallas kernels, local_decode(): pl.pallas_call(functools.partial(kernel, rows_n, cols_n), out_shape=jax.S...  114 us

profile of v4, /device:TPU:0, one launch (start us, length us, event | category | flops | bytes accessed | tf_op | source)
XLA Modules:
  0.0 116.8 jit_solution(15927747156034123644)
XLA Ops:
  0.0 0.7 convert_element_type.3
  0.7 114.3 %decode.1 = f32[16,3,16,96]{3,2,1,0:T(8,128)} custom-call(bf16[16,96,16,256]{3,2,1,0:T(8,128)(2,1)} %act_in.1, bf16[2,256]{1,0:T(2,128)(2,1)} %norm_first.1, bf16[3,3,256,128]{3,2,1,0:T(8,128)(2,1)} %w_first.1, bf16[256,128]{1,0:T(8,128)(2,1)} %w_short.1, bf16[6,2,128]{2,1,0:T(2,128)(2,1)} %norm_rest.1, bf16[5,3,3,128,128]{4,3,2,1,0:T(8,128)(2,1)} %w_rest.1, ...), custom_call_target="tpu_custom_call" | custom-call | tf_op jit(solution)/shard_map/decode/pallas_call | solution.py:460
  114.9 1.8 %add_bitcast_fusion = f32[16,96,16,3]{1,2,3,0:T(8,128)} fusion(f32[16,3,16,96]{3,2,1,0:T(8,128)} %decode.1, f32[3]{0:T(128)S(1)} %convert_element_type.3), kind=kLoop, calls=%fused_computation | loop fusion | flops 73728 | bytes 589836 | tf_op jit(solution)/shard_map/add | solution.py:507

commit v5 on v4

--- a/solution.py
+++ b/solution.py
@@ -17,14 +17,20 @@
 SIDE = 512
 DEEP = 1024
 PAIR = (0, 1)
+ZERO = 0.0
 BF16 = jnp.bfloat16
 SLAB = 48
 BLOCK = 8
 STEPS = SLAB // BLOCK
 EARLY = 4
+SENT = 24
 CHUNK = 4
 DEPTH = 8
 CHUNKS = SLAB // CHUNK
+
+
+def over_groups(body):
+    lax.fori_loop(0, 2, body, 0)
 
 
 def exact_rows(values):
@@ -52,7 +58,7 @@
 def kernel(rows_n, cols_n, act_in, norm_first, w_first, w_short, norm_rest, w_rest, bias_rest, w_out, image,
            flat, order, bias_f, stage, raw_a, raw_t, raw_h, act_a0, act_a1, act_a2, act_t0, act_t1, act_t2, wf, wfs, ws, wr, wrs, wo, perm, sum_a, sum_t, cast_a, cast_t,
            col_a, row_a, cor_a, col_t, row_t, cor_t, slots,
-           in_sem, wt_sem, col_send, col_recv, row_send, row_recv, cor_send, cor_recv, stat_send, stat_recv):
+           in_sem, wt_sem, col_send, col_recv, row_send, row_recv, cor_send, cor_recv, stat_send, stat_recv, ready):
     peers = rows_n * cols_n
     act_a = (act_a0, act_a1, act_a2)
     act_t = (act_t0, act_t1, act_t2)
@@ -104,11 +110,8 @@
     def send_sums(par, g, message):
         slots[par, g, me] = message
 
-        def one(offset, carry):
+        for offset in sorted(range(1, peers), key=lambda offset: -min(offset, peers - offset)):
             stat_copy(par, g, offset).start()
-            return carry
-
-        lax.fori_loop(1, peers, one, 0)
 
     def finish_exchange(raw, col, row, cor, par, g):
         for side in PAIR:
@@ -160,7 +163,7 @@
             ring[local:local + size, 1:9, 0] = out[:, :, 1]
             for side in PAIR:
                 edge = activate(col[par, g, side, first:first + size], scale, shift)
-                ring[local:local + size, 8 * side, side] = jnp.where(has_side[side], edge, 0.0).astype(BF16)
+                ring[local:local + size, 8 * side, side] = jnp.where(has_side[side], edge, ZERO).astype(BF16)
 
         def outer_row(ring, local, end):
             inner = SLAB - 1 if end == 0 else 0
@@ -171,8 +174,8 @@
                 near = activate(mine.astype(F32)[..., own, :], scale[0:8], shift[0:8])
                 away = activate(theirs.astype(F32)[..., far, :], scale[0:8], shift[0:8])
                 if mine_present is not None:
-                    near = jnp.where(mine_present, near, 0.0)
-                away = jnp.where(theirs_present, away, 0.0)
+                    near = jnp.where(mine_present, near, ZERO)
+                away = jnp.where(theirs_present, away, ZERO)
                 return jnp.concatenate([away, near] if end == 0 else [near, away], axis=-2).astype(BF16)
 
             line = join(raw[g, inner], row[par, g, end], None, has_end[end])
@@ -235,10 +238,10 @@
             dst[g, span, :, 1] = tiles[..., LANES:]
             chunk(step + 1)
             if step == EARLY - 1:
-                send_cols(dst, col, par, g, 0, EARLY * BLOCK)
+                send_cols(dst, col, par, g, 0, SENT)
         send_sums(par, g, message_of(sum_one[:, :LANES] + sum_one[:, LANES:], sum_two[:, :LANES] + sum_two[:, LANES:], sum_t[...]))
         send_ends(dst, row, cor, par, g)
-        send_cols(dst, col, par, g, EARLY * BLOCK, SLAB - EARLY * BLOCK)
+        send_cols(dst, col, par, g, SENT, SLAB - SENT)
 
     def input_copy(g, chunk, half):
         index = g * CHUNKS + chunk
@@ -252,11 +255,25 @@
 
     barrier = pltpu.get_barrier_semaphore()
 
-    def greet(offset, carry):
-        pl.semaphore_signal(barrier, inc=1, device_id=peer(lax.rem(me + offset, peers)), device_id_type=MESH)
-        return carry
-
-    lax.fori_loop(1, peers, greet, 0)
+    beside = 1 + sum(flag.astype(jnp.int32) for flag in has_side)
+    around = beside * (1 + sum(flag.astype(jnp.int32) for flag in has_end)) - 1
+
+    def greet(semaphore):
+        for side in PAIR:
+            @pl.when(has_side[side])
+            def _():
+                pl.semaphore_signal(semaphore, inc=1, device_id=at(2 * side - 1, 0), device_id_type=MESH)
+        for end in PAIR:
+            @pl.when(has_end[end])
+            def _():
+                pl.semaphore_signal(semaphore, inc=1, device_id=at(0, 2 * end - 1), device_id_type=MESH)
+            for side in PAIR:
+                @pl.when(jnp.logical_and(has_end[end], has_side[side]))
+                def _():
+                    pl.semaphore_signal(semaphore, inc=1, device_id=at(2 * side - 1, 2 * end - 1), device_id_type=MESH)
+
+    rounds = max(rows_n, cols_n) - 1
+    greet(barrier)
 
     out_row = lax.broadcasted_iota(jnp.int32, (WIDE, WIDE), 0)
     in_row = lax.broadcasted_iota(jnp.int32, (WIDE, WIDE), 1)
@@ -338,7 +355,16 @@
 
             @pl.when(index == 1)
             def _():
-                pl.semaphore_wait(barrier, peers - 1)
+                pl.semaphore_wait(barrier, around)
+                if rounds > 1:
+                    greet(ready.at[0])
+
+            for later_round in range(1, rounds):
+                @pl.when(index == 1 + 4 * later_round)
+                def _():
+                    pl.semaphore_wait(ready.at[later_round - 1], around)
+                    if later_round < rounds - 1:
+                        greet(ready.at[later_round])
 
             @pl.when(chunk > 0)
             def _():
@@ -353,7 +379,7 @@
         send_ends(raw_a, row_a, cor_a, 0, g)
         return carry
 
-    lax.fori_loop(0, 2, load_group, 0)
+    over_groups(load_group)
     for copy in weight_copies(False):
         copy.start()
     for copy in weight_copies(True):
@@ -369,7 +395,7 @@
         convolve(act_a, chunk, WIDE, lambda: (wf[...].reshape(1536, WIDE), wfs[0].reshape(DEEP, WIDE), wfs[1].reshape(DEEP, WIDE)), bias_row(0), raw_t, col_t, row_t, cor_t, 1, g)
         return carry
 
-    lax.fori_loop(0, 2, first_conv, 0)
+    over_groups(first_conv)
     for copy in weight_copies(False):
         copy.wait()
 
@@ -394,7 +420,7 @@
         layer(raw_t, 0, weights, bias_row(1) + bias_row(6), raw_h, 1, g, extra=extra)
         return carry
 
-    lax.fori_loop(0, 2, shortcut_conv, 0)
+    over_groups(shortcut_conv)
 
     def resnet(res, carry):
         base = 2 * res + 1
@@ -407,11 +433,11 @@
             layer(raw_t, base + 1, lambda: (wr[base + 1].reshape(768, WIDE), *side_weights(base + 1)), bias_row(base + 2), raw_h, 1, g, residual=raw_h)
             return inner
 
-        lax.fori_loop(0, 2, first_half, 0)
-        lax.fori_loop(0, 2, second_half, 0)
+        over_groups(first_half)
+        over_groups(second_half)
         return carry
 
-    lax.fori_loop(0, 2, resnet, 0)
+    over_groups(resnet)
 
     def out_conv(g, carry):
         chunk = layer(raw_h, 5, None, None, None, 0, g)
@@ -444,7 +470,7 @@
             image[pl.ds(g * 8, 8), channel] = total.reshape(8, SUB, 2 * SLAB)
         return carry
 
-    lax.fori_loop(0, 2, out_conv, 0)
+    over_groups(out_conv)
 
 
 def solution(mesh):
@@ -500,6 +526,7 @@
                 dma((2, 2, 2, 2)),
                 dma((2, 2)),
                 dma((2, 2)),
+                pltpu.SemaphoreType.REGULAR((max(rows_n, cols_n),)),
             ],
             compiler_params=pltpu.CompilerParams(collective_id=0, has_side_effects=True, vmem_limit_bytes=62 << 20),
             name="decode",

time: 117 us -> 115 us (0.983)
  Pallas kernels: 114 us -> 112 us
    pallas_call x1, Pallas kernels: 114 us -> 112 us  [local_decode(): pl.pallas_call(functools.partial(kernel, rows_n, cols_n), out_shape=jax.S...]
where the time goes in v5:
time: 115 us; the launch traced here: 114 us
  Pallas kernels  112 us (97%)
  other arithmetic  2.49 us (2%)
    pallas_call x1, Pallas kernels, local_decode(): pl.pallas_call(functools.partial(kernel, rows_n, cols_n), out_shape=jax.S...  112 us

profile of v5, /device:TPU:0, one launch (start us, length us, event | category | flops | bytes accessed | tf_op | source)
XLA Modules:
  0.0 114.5 jit_solution(16634240707589946096)
XLA Ops:
  0.0 0.7 convert_element_type.3
  0.7 112.0 %decode.1 = f32[16,3,16,96]{3,2,1,0:T(8,128)} custom-call(bf16[16,96,16,256]{3,2,1,0:T(8,128)(2,1)} %act_in.1, bf16[2,256]{1,0:T(2,128)(2,1)} %norm_first.1, bf16[3,3,256,128]{3,2,1,0:T(8,128)(2,1)} %w_first.1, bf16[256,128]{1,0:T(8,128)(2,1)} %w_short.1, bf16[6,2,128]{2,1,0:T(2,128)(2,1)} %norm_rest.1, bf16[5,3,3,128,128]{4,3,2,1,0:T(8,128)(2,1)} %w_rest.1, ...), custom_call_target="tpu_custom_call" | custom-call | tf_op jit(solution)/shard_map/decode/pallas_call | solution.py:486
  112.6 1.8 %add_bitcast_fusion = f32[16,96,16,3]{1,2,3,0:T(8,128)} fusion(f32[16,3,16,96]{3,2,1,0:T(8,128)} %decode.1, f32[3]{0:T(128)S(1)} %convert_element_type.3), kind=kLoop, calls=%fused_computation | loop fusion | flops 73728 | bytes 589836 | tf_op jit(solution)/shard_map/add | solution.py:534
